TPU v7x, 256 devices: a whole 4x4x8 slice. The times are simulated.
256 devices in a mesh: dp: 64 (over x, y, z_hi, core), mp: 4 (over z_lo).
Axes of the slice: x: 4, y: 4, z: 8 (z_hi: 2, z_lo: 4; z = z_hi * 4 + z_lo), core: 2. Of those that a mesh axis runs over, the one named last changes fastest.
Arguments:
- states: bfloat16 [1024, 80, 768], P('dp'), may hold values from -16 to 16
- hist_len: int32 [1024], P('dp'), may hold values from 1 to 20
- norm_gain: float32 [768], replicated, may hold values from 0.5 to 1.5
- qkv_weight: bfloat16 [768, 3, 12, 64], P(None, None, 'mp'), may hold values from -1 to 1
- output_weight: bfloat16 [12, 64, 768], P('mp'), may hold values from -0.21875 to 0.21875
- cotangent: bfloat16 [1024, 80, 768], P('dp'), may hold values from -16 to 16
Outputs:
- attended: bfloat16 [1024, 80, 768], P('dp')
- grad_states: bfloat16 [1024, 80, 768], P('dp')
- grad_qkv: float32 [768, 3, 12, 64], P('dp', None, 'mp')
- output_weight_gradient: float32 [12, 64, 768], P('mp', None, 'dp')
- grad_gain: float32 [768], P('dp')
All inputs are finite; a program needn't handle non-finite values.
Results may differ from a plain program's by a relative error of at most 0.012.
Values may be sent and summed in bfloat16 or wider, within the bound.
A program may use at most 128 MiB of HBM per device.

v0:
```python
import jax
import jax.numpy as jnp
from jax import lax
from jax.sharding import PartitionSpec as P

LEVELS = 4


def cut_along(shard, dim, count):
    shape = shard.shape
    tiles = shard.reshape(*shape[:dim], count, shape[dim] // count, *shape[dim + 1 :])
    return jnp.moveaxis(tiles, dim, 0)


def summed_on_arrival(shard, axis, dim):
    count = lax.axis_size(axis)
    tiles = lax.all_to_all(cut_along(shard, dim, count), axis, 0, 0, tiled=True)
    return jnp.sum(tiles.astype(jnp.float32), axis=0)


def joined_along(tiles, dim):
    shape = list(tiles.shape[1:])
    shape[dim] *= tiles.shape[0]
    return jnp.moveaxis(tiles, 0, dim).reshape(shape)


def from_everyone(shard, axis):
    copies = jnp.broadcast_to(shard, (lax.axis_size(axis), *shard.shape))
    return lax.all_to_all(copies, axis, split_axis=0, concat_axis=0, tiled=True)


def gather_directly(shard, axis, dim):
    return joined_along(from_everyone(shard, axis), dim)


def of_everyone(shard, axis):
    everything = from_everyone(shard, axis)
    return jnp.sum(everything, axis=0)


def body(states, hist_len, norm_gain, qkv_weight, output_weight, cotangent):
    width = states.shape[2]
    share_width = width // lax.axis_size("mp")
    offset = lax.axis_index("mp") * share_width
    wide_states = states.astype(jnp.float32)
    inv_rms = lax.rsqrt(jnp.mean(wide_states * wide_states, axis=-1, keepdims=True) + 1e-06)
    unit = wide_states * inv_rms
    normed = (unit * norm_gain).astype(jnp.bfloat16)
    proj = jnp.einsum(
        "bsd,dchk->bschk", normed, qkv_weight, preferred_element_type=jnp.float32
    ).astype(jnp.bfloat16)
    queries = proj[:, :, 0]
    key_rows = proj[:, :, 1]
    value_rows = proj[:, :, 2]
    positions = jnp.arange(states.shape[1], dtype=jnp.int32)
    keep_mask = positions[None, :] < LEVELS * hist_len[:, None]
    scores = jnp.einsum("bqhk,bphk->bhqp", queries, key_rows, preferred_element_type=jnp.float32)
    masked = jnp.where(keep_mask[:, None, None, :], scores, -1e30)
    row_top = jnp.max(masked, axis=-1, keepdims=True)
    exp_scores = jnp.exp(masked - row_top)
    attn_prob = exp_scores / jnp.sum(exp_scores, axis=-1, keepdims=True)
    prob_bf = attn_prob.astype(jnp.bfloat16)
    attended_context = jnp.einsum(
        "bhqp,bphk->bqhk", prob_bf, value_rows, preferred_element_type=jnp.float32
    ).astype(jnp.bfloat16)
    partial_mix = jnp.einsum(
        "zagm,gms->zas", attended_context, output_weight, preferred_element_type=jnp.float32
    )
    mixed_share = summed_on_arrival(partial_mix.astype(jnp.bfloat16), "mp", 2)
    states_slice = lax.dynamic_slice_in_dim(wide_states, offset, share_width, 2)
    attended_share = (states_slice + mixed_share).astype(jnp.bfloat16)
    attended = gather_directly(attended_share, "mp", 2)
    masked_cotangent = jnp.where(keep_mask[:, :, None], cotangent, jnp.zeros_like(cotangent))
    local_output = jnp.einsum(
        "wmep,wmx->epx", attended_context, masked_cotangent, preferred_element_type=jnp.float32
    )
    context_gradient = jnp.einsum(
        "uxy,wgy->uxwg", masked_cotangent, output_weight, preferred_element_type=jnp.float32
    ).astype(jnp.bfloat16)
    grad_prob = jnp.einsum(
        "bqhk,bphk->bhqp", context_gradient, value_rows, preferred_element_type=jnp.float32
    )
    row_delta = jnp.sum(attn_prob * grad_prob, axis=-1, keepdims=True)
    grad_score = (attn_prob * (grad_prob - row_delta)).astype(jnp.bfloat16)
    grad_query = jnp.einsum(
        "bhqp,bphk->bqhk", grad_score, key_rows, preferred_element_type=jnp.float32
    )
    grad_key = jnp.einsum(
        "bhqp,bqhk->bphk", grad_score, queries, preferred_element_type=jnp.float32
    )
    grad_value = jnp.einsum(
        "bhqp,bqhk->bphk", prob_bf, context_gradient, preferred_element_type=jnp.float32
    )
    grad_proj = jnp.stack([grad_query, grad_key, grad_value], axis=2).astype(jnp.bfloat16)
    local_qkv = jnp.einsum("bsd,bschk->dchk", normed, grad_proj, preferred_element_type=jnp.float32)
    partial_normed = jnp.einsum(
        "bschk,dchk->bsd", grad_proj, qkv_weight, preferred_element_type=jnp.float32
    )
    wide_cot = masked_cotangent.astype(jnp.float32)
    normed_share = summed_on_arrival(partial_normed.astype(jnp.bfloat16), "mp", 2)
    unit_share = lax.dynamic_slice_in_dim(unit, offset, share_width, 2)
    gain_share = lax.dynamic_slice_in_dim(norm_gain, offset, share_width, 0)
    cot_share = lax.dynamic_slice_in_dim(wide_cot, offset, share_width, 2)
    unit_grad = normed_share * gain_share
    row_sums = of_everyone(jnp.sum(unit_grad * unit_share, axis=-1, keepdims=True), "mp")
    states_share = (cot_share + inv_rms * (unit_grad - unit_share * (row_sums / width))).astype(
        jnp.bfloat16
    )
    grad_states = gather_directly(states_share, "mp", 2)
    gain_share_grad = jnp.sum(normed_share * unit_share, axis=(0, 1))
    local_gain = gather_directly(gain_share_grad, "mp", 0)
    grad_qkv, output_weight_gradient, grad_gain = (
        summed_on_arrival(local_qkv.astype(jnp.bfloat16), "dp", 0),
        summed_on_arrival(local_output.astype(jnp.bfloat16), "dp", 2),
        summed_on_arrival(local_gain.astype(jnp.bfloat16), "dp", 0),
    )
    return (attended, grad_states, grad_qkv, output_weight_gradient, grad_gain)


def solution(mesh):
    placed = (
        P("dp", None, None),
        P("dp"),
        P(),
        P(None, None, "mp", None),
        P("mp", None, None),
        P("dp", None, None),
    )
    return jax.shard_map(
        body,
        mesh=mesh,
        in_specs=placed,
        out_specs=(
            P("dp", None, None),
            P("dp", None, None),
            P("dp", None, "mp", None),
            P("mp", None, "dp"),
            P("dp"),
        ),
        check_vma=False,
    )
```

profile of v0, /device:TPU:1, one launch (start us, length us, event | category | flops | bytes accessed | tf_op | source)
XLA Modules:
  0.0 414.7 jit_solution(8543157783831194893)
XLA Ops:
  3.1 3.4 convolution_convert_fusion
  6.5 3.6 fusion.37
  23.8 15.6 %all-to-all-start.6 = ((bf16[64,2,1152]{2,1,0:T(2,128)(2,1)}), bf16[64,2,1152]{2,1,0:T(2,128)(2,1)S(1)}, u32[]{:S(2)}, u32[]{:S(2)}) async-start(bf16[64,2,1152]{2,1,0:T(2,128)(2,1)} %reshape.122), calls=%async_computation.6 | async-start | bytes 589824 | tf_op jit(solution)/shard_map/all_to_all | solution.py:17
  50.3 6.2 %reshape.107 = bf16[16,80,4,192]{3,2,1,0:T(4,128)(2,1)} reshape(bf16[16,80,768]{2,1,0:T(8,128)(2,1)} %bitcast_convert_fusion) | data formatting | bytes 3932160 | tf_op jit(solution)/shard_map/reshape | solution.py:11
  56.5 3.6 copy.91
  60.1 4.5 %all-to-all-start.2 = ((bf16[4,16,80,192]{3,2,1,0:T(8,128)(2,1)}), bf16[4,16,80,192]{3,2,1,0:T(8,128)(2,1)}, u32[]{:S(2)}, u32[]{:S(2)}) async-start(bf16[4,16,80,192]{3,2,1,0:T(8,128)(2,1)} %bitcast.129), calls=%async_computation.2 | async-start | bytes 5242880 | tf_op jit(solution)/shard_map/all_to_all | solution.py:17
  64.7 3.3 bitcast_convert_fusion.2
  69.7 4.1 reshape.109
  73.8 3.5 copy.93
  77.3 4.7 %reshape.120 = bf16[64,2,3456]{2,1,0:T(2,128)(2,1)} reshape(bf16[64,3,3,12,64]{4,3,2,1,0:T(8,128)(2,1)} %bitcast.131) | data formatting | bytes 1769472
  82.0 41.7 %all-to-all-done.2 = bf16[4,16,80,192]{3,2,1,0:T(8,128)(2,1)} async-done(((bf16[4,16,80,192]{3,2,1,0:T(8,128)(2,1)}), bf16[4,16,80,192]{3,2,1,0:T(8,128)(2,1)}, u32[]{:S(2)}, u32[]{:S(2)}) %all-to-all-start.2) | async-done | bytes 1966112 | tf_op jit(solution)/shard_map/all_to_all | solution.py:17
  123.7 13.8 %all-to-all-start.5 = ((bf16[64,2,3456]{2,1,0:T(2,128)(2,1)}), bf16[64,2,3456]{2,1,0:T(2,128)(2,1)S(1)}, u32[]{:S(2)}, u32[]{:S(2)}) async-start(bf16[64,2,3456]{2,1,0:T(2,128)(2,1)} %reshape.120), calls=%async_computation.5 | async-start | bytes 1769472 | tf_op jit(solution)/shard_map/all_to_all | solution.py:17
  138.0 3.7 convert_reduce_fusion
  143.6 21.2 %all-to-all-done.5 = bf16[64,2,3456]{2,1,0:T(2,128)(2,1)S(1)} async-done(((bf16[64,2,3456]{2,1,0:T(2,128)(2,1)}), bf16[64,2,3456]{2,1,0:T(2,128)(2,1)S(1)}, u32[]{:S(2)}, u32[]{:S(2)}) %all-to-all-start.5) | async-done | bytes 884768 | tf_op jit(solution)/shard_map/all_to_all | solution.py:17
  165.4 3.2 all-to-all-start.7
  168.7 3.2 bitcast_convert_fusion.1
  171.9 6.2 %reshape.105 = bf16[16,80,4,192]{3,2,1,0:T(4,128)(2,1)} reshape(bf16[16,80,768]{2,1,0:T(8,128)(2,1)} %bitcast_convert_fusion.1) | data formatting | bytes 3932160 | tf_op jit(solution)/shard_map/reshape | solution.py:11
  178.1 3.7 copy.92
  181.8 4.6 %all-to-all-start = ((bf16[4,16,80,192]{3,2,1,0:T(8,128)(2,1)}), bf16[4,16,80,192]{3,2,1,0:T(8,128)(2,1)}, u32[]{:S(2)}, u32[]{:S(2)}) async-start(bf16[4,16,80,192]{3,2,1,0:T(8,128)(2,1)} %bitcast.130), calls=%async_computation | async-start | bytes 5242880 | tf_op jit(solution)/shard_map/all_to_all | solution.py:17
  189.4 56.0 %all-to-all-done = bf16[4,16,80,192]{3,2,1,0:T(8,128)(2,1)} async-done(((bf16[4,16,80,192]{3,2,1,0:T(8,128)(2,1)}), bf16[4,16,80,192]{3,2,1,0:T(8,128)(2,1)}, u32[]{:S(2)}, u32[]{:S(2)}) %all-to-all-start) | async-done | bytes 1966112 | tf_op jit(solution)/shard_map/all_to_all | solution.py:17
  245.4 7.5 %all-to-all-start.8 = ((bf16[64,1,12]{2,1,0:T(2,128)(2,1)}), bf16[64,1,12]{2,1,0:T(2,128)(2,1)S(1)}, u32[]{:S(2)}, u32[]{:S(2)}) async-start(bf16[64,1,12]{2,1,0:T(2,128)(2,1)} %convert_element_type.98), calls=%async_computation.8 | async-start | bytes 65536 | tf_op jit(solution)/shard_map/all_to_all | solution.py:17
  255.2 9.3 %all-to-all-done.8 = bf16[64,1,12]{2,1,0:T(2,128)(2,1)S(1)} async-done(((bf16[64,1,12]{2,1,0:T(2,128)(2,1)}), bf16[64,1,12]{2,1,0:T(2,128)(2,1)S(1)}, u32[]{:S(2)}, u32[]{:S(2)}) %all-to-all-start.8) | async-done | bytes 1568 | tf_op jit(solution)/shard_map/all_to_all | solution.py:17
  265.1 3.3 all-to-all-start.3
  274.6 4.7 %all-to-all-start.1 = ((bf16[4,16,80,192]{3,2,1,0:T(8,128)(2,1)}), bf16[4,16,80,192]{3,2,1,0:T(8,128)(2,1)}, u32[]{:S(2)}, u32[]{:S(2)}) async-start(bf16[4,16,80,192]{3,2,1,0:T(8,128)(2,1)} %broadcast_in_dim.48), calls=%async_computation.1 | async-start | bytes 5242880 | tf_op jit(solution)/shard_map/all_to_all | solution.py:29
  282.1 56.2 %all-to-all-done.1 = bf16[4,16,80,192]{3,2,1,0:T(8,128)(2,1)} async-done(((bf16[4,16,80,192]{3,2,1,0:T(8,128)(2,1)}), bf16[4,16,80,192]{3,2,1,0:T(8,128)(2,1)}, u32[]{:S(2)}, u32[]{:S(2)}) %all-to-all-start.1) | async-done | bytes 1966112 | tf_op jit(solution)/shard_map/all_to_all | solution.py:29
  340.1 4.8 %all-to-all-start.4 = ((bf16[4,16,80,192]{3,2,1,0:T(8,128)(2,1)}), bf16[4,16,80,192]{3,2,1,0:T(8,128)(2,1)}, u32[]{:S(2)}, u32[]{:S(2)}) async-start(bf16[4,16,80,192]{3,2,1,0:T(8,128)(2,1)} %broadcast_in_dim.52), calls=%async_computation.4 | async-start | bytes 5242880 | tf_op jit(solution)/shard_map/all_to_all | solution.py:29
  346.1 3.6 reshape.121
  351.6 3.8 copy.59
  355.4 3.3 reshape.106
  358.7 45.0 %all-to-all-done.4 = bf16[4,16,80,192]{3,2,1,0:T(8,128)(2,1)} async-done(((bf16[4,16,80,192]{3,2,1,0:T(8,128)(2,1)}), bf16[4,16,80,192]{3,2,1,0:T(8,128)(2,1)}, u32[]{:S(2)}, u32[]{:S(2)}) %all-to-all-start.4) | async-done | bytes 1966112 | tf_op jit(solution)/shard_map/all_to_all | solution.py:29
  403.7 5.4 %copy.64 = bf16[16,80,4,192]{3,2,1,0:T(4,128)(2,1)} copy(bf16[16,80,4,192]{3,1,0,2:T(8,128)(2,1)} %bitcast.24) | data formatting | bytes 3932160 | tf_op jit(solution)/shard_map/transpose | solution.py:24
  409.0 5.7 %reshape.108 = bf16[16,80,768]{2,1,0:T(8,128)(2,1)} reshape(bf16[16,80,4,192]{3,2,1,0:T(4,128)(2,1)} %copy.64) | data formatting | bytes 3932160 | tf_op jit(solution)/shard_map/reshape | solution.py:24
  (77 shorter events, 51.4 us)
Async XLA Ops:
  0.6 2.3 copy-start
  0.6 2.4 copy-start.2
  0.7 2.2 copy-start.16
  0.7 2.4 copy-start.15
  10.1 2.1 copy-start.8
  12.0 2.3 copy-start.7
  14.3 0.9 copy-start.11
  19.0 20.4 %copy-start.14 = (bf16[3,64,768]{2,1,0:T(8,128)(2,1)S(1)}, bf16[3,64,768]{2,1,0:T(8,128)(2,1)}, u32[]{:S(2)}) copy-start(bf16[3,64,768]{2,1,0:T(8,128)(2,1)} %param.10) | copy-start | bytes 884740
  23.8 36.4 %all-to-all-start.6 = ((bf16[64,2,1152]{2,1,0:T(2,128)(2,1)}), bf16[64,2,1152]{2,1,0:T(2,128)(2,1)S(1)}, u32[]{:S(2)}, u32[]{:S(2)}) async-start(bf16[64,2,1152]{2,1,0:T(2,128)(2,1)} %reshape.122), calls=%async_computation.6 | async-start | bytes 589824 | tf_op jit(solution)/shard_map/all_to_all | solution.py:17
  39.4 2.6 copy-start.9
  42.0 1.7 copy-start.10
  43.6 2.1 copy-start.17
  45.3 0.9 copy-start.12
  46.2 0.9 copy-start.13
  60.1 63.6 %all-to-all-start.2 = ((bf16[4,16,80,192]{3,2,1,0:T(8,128)(2,1)}), bf16[4,16,80,192]{3,2,1,0:T(8,128)(2,1)}, u32[]{:S(2)}, u32[]{:S(2)}) async-start(bf16[4,16,80,192]{3,2,1,0:T(8,128)(2,1)} %bitcast.129), calls=%async_computation.2 | async-start | bytes 5242880 | tf_op jit(solution)/shard_map/all_to_all | solution.py:17
  123.7 41.0 %all-to-all-start.5 = ((bf16[64,2,3456]{2,1,0:T(2,128)(2,1)}), bf16[64,2,3456]{2,1,0:T(2,128)(2,1)S(1)}, u32[]{:S(2)}, u32[]{:S(2)}) async-start(bf16[64,2,3456]{2,1,0:T(2,128)(2,1)} %reshape.120), calls=%async_computation.5 | async-start | bytes 1769472 | tf_op jit(solution)/shard_map/all_to_all | solution.py:17
  138.0 3.7 copy-start.5
  141.7 1.1 copy-start.3
  164.8 13.3 %copy-start.6 = (bf16[64,2,3456]{2,1,0:T(2,128)(2,1)}, bf16[64,2,3456]{2,1,0:T(2,128)(2,1)S(1)}, u32[]{:S(2)}) copy-start(bf16[64,2,3456]{2,1,0:T(2,128)(2,1)S(1)} %all-to-all-done.5) | copy-start | bytes 2654212
  165.4 16.4 %all-to-all-start.7 = ((bf16[4,1,192]{2,1,0:T(2,128)(2,1)}), bf16[4,1,192]{2,1,0:T(2,128)(2,1)S(1)}, u32[]{:S(2)}, u32[]{:S(2)}) async-start(bf16[4,1,192]{2,1,0:T(2,128)(2,1)} %broadcast_in_dim.53), calls=%async_computation.7 | async-start | bytes 8192 | tf_op jit(solution)/shard_map/all_to_all | solution.py:29
  181.8 63.6 %all-to-all-start = ((bf16[4,16,80,192]{3,2,1,0:T(8,128)(2,1)}), bf16[4,16,80,192]{3,2,1,0:T(8,128)(2,1)}, u32[]{:S(2)}, u32[]{:S(2)}) async-start(bf16[4,16,80,192]{3,2,1,0:T(8,128)(2,1)} %bitcast.130), calls=%async_computation | async-start | bytes 5242880 | tf_op jit(solution)/shard_map/all_to_all | solution.py:17
  245.4 19.1 %all-to-all-start.8 = ((bf16[64,1,12]{2,1,0:T(2,128)(2,1)}), bf16[64,1,12]{2,1,0:T(2,128)(2,1)S(1)}, u32[]{:S(2)}, u32[]{:S(2)}) async-start(bf16[64,1,12]{2,1,0:T(2,128)(2,1)} %convert_element_type.98), calls=%async_computation.8 | async-start | bytes 65536 | tf_op jit(solution)/shard_map/all_to_all | solution.py:17
  265.1 7.7 %all-to-all-start.3 = ((f32[4,16,80,1]{2,1,3,0:T(8,128)}), f32[4,16,80,1]{2,1,3,0:T(8,128)S(1)}, u32[]{:S(2)}, u32[]{:S(2)}) async-start(f32[4,16,80,1]{2,1,3,0:T(8,128)} %broadcast_in_dim.51), calls=%async_computation.3 | async-start | bytes 65536 | tf_op jit(solution)/shard_map/all_to_all | solution.py:29
  274.6 4.7 %copy-start.4 = (f32[16,80,192]{2,1,0:T(8,128)S(1)}, f32[16,80,192]{2,1,0:T(8,128)}, u32[]{:S(2)}) copy-start(f32[16,80,192]{2,1,0:T(8,128)} %copy-done.3) | copy-start | bytes 2949124
  274.6 63.7 %all-to-all-start.1 = ((bf16[4,16,80,192]{3,2,1,0:T(8,128)(2,1)}), bf16[4,16,80,192]{3,2,1,0:T(8,128)(2,1)}, u32[]{:S(2)}, u32[]{:S(2)}) async-start(bf16[4,16,80,192]{3,2,1,0:T(8,128)(2,1)} %broadcast_in_dim.48), calls=%async_computation.1 | async-start | bytes 5242880 | tf_op jit(solution)/shard_map/all_to_all | solution.py:29
  340.1 63.6 %all-to-all-start.4 = ((bf16[4,16,80,192]{3,2,1,0:T(8,128)(2,1)}), bf16[4,16,80,192]{3,2,1,0:T(8,128)(2,1)}, u32[]{:S(2)}, u32[]{:S(2)}) async-start(bf16[4,16,80,192]{3,2,1,0:T(8,128)(2,1)} %broadcast_in_dim.52), calls=%async_computation.4 | async-start | bytes 5242880 | tf_op jit(solution)/shard_map/all_to_all | solution.py:29
  403.7 11.0 %copy-start.1 = (bf16[768,3,3,64]{0,3,2,1:T(8,128)(2,1)S(1)}, bf16[768,3,3,64]{0,3,2,1:T(8,128)(2,1)}, u32[]{:S(2)}) copy-start(bf16[768,3,3,64]{0,3,2,1:T(8,128)(2,1)} %param.9) | copy-start | bytes 2654212
where the time goes:
time: 416 us; the launch traced here: 415 us
  waiting for transfers between devices  232 us (56%)
  local copies, waits for them, and re-layouts  73.3 us (18%)
  starting transfers between devices  61.9 us (15%)
  matrix products  25 us (6%)
  other arithmetic  21.6 us (5%)
    all_to_all x5, waiting for transfers between devices, summed_on_arrival(): tiles = lax.all_to_all(cut_along(shard, dim, count), axis, 0, 0, tiled=True)  128 us
    all_to_all x4, waiting for transfers between devices, from_everyone(): return lax.all_to_all(copies, axis, split_axis=0, concat_axis=0, tiled=True)  104 us
    all_to_all x5, starting transfers between devices, summed_on_arrival(): tiles = lax.all_to_all(cut_along(shard, dim, count), axis, 0, 0, tiled=True)  45.9 us
    reshape x7, local copies, waits for them, and re-layouts, cut_along(): shard.reshape(*shape[:dim], count, shape[dim] // count, *shape[dim + 1:])  28.4 us
    unnamed x41, local copies, waits for them, and re-layouts  18.2 us
    all_to_all x4, starting transfers between devices, from_everyone(): return lax.all_to_all(copies, axis, split_axis=0, concat_axis=0, tiled=True)  16 us
    transpose x2, local copies, waits for them, and re-layouts, joined_along(): return jnp.moveaxis(tiles, 0, dim).reshape(shape)  9.13 us
    reshape x2, local copies, waits for them, and re-layouts, joined_along(): return jnp.moveaxis(tiles, 0, dim).reshape(shape)  8.97 us
  transfers between devices with their start and end apart: 9, of which 7 were waited for; matrix products, arithmetic and copies ran while one was open for 19% of the time, Pallas kernels for 0%

commit v1 on v0

v1 whole, which is shorter than its diff:
```python
import jax, jax.numpy as jnp
from jax import lax
from jax.experimental import pallas as pl
from jax.experimental.pallas import tpu as pltpu
from jax.sharding import PartitionSpec as P

S=80; D=768; NB=4; R=NB*S
f32=jnp.float32; bf16=jnp.bfloat16

def nt(a,b): return lax.dot_general(a,b,(((1,),(1,)),((),())),preferred_element_type=f32)
def nn(a,b): return lax.dot_general(a,b,(((1,),(0,)),((),())),preferred_element_type=f32)
def tn(a,b): return lax.dot_general(a,b,(((0,),(0,)),((),())),preferred_element_type=f32)

def attend(q,k,v,dc,keys):
    lane=lax.broadcasted_iota(jnp.int32,(1,256),1)//64
    ms=[(lane==h).astype(bf16) for h in range(3)]
    mf=[m.astype(f32) for m in ms]
    z=jnp.zeros((16,256),bf16)
    qs=jnp.concatenate([q*m for m in ms]+[z],axis=0)
    dst=jnp.concatenate([dc*m for m in ms]+[z],axis=0)
    st=nt(k,qs)
    keep=lax.broadcasted_iota(jnp.int32,(S,256),0)<keys
    st=jnp.where(keep,st,-1e30)
    e=jnp.exp(st-jnp.max(st,axis=0,keepdims=True))
    p=e*(1.0/jnp.sum(e,axis=0,keepdims=True))
    pb=p.astype(bf16)
    o=tn(pb,v)
    ctx=o[0:S]*mf[0]+o[S:2*S]*mf[1]+o[2*S:3*S]*mf[2]
    dp=nt(v,dst)
    ds=(p*(dp-jnp.sum(p*dp,axis=0,keepdims=True))).astype(bf16)
    dv=nn(pb,dst)
    dk=nn(ds,qs)
    u=tn(ds,k)
    dq=u[0:S]*mf[0]+u[S:2*S]*mf[1]+u[2*S:3*S]*mf[2]
    return ctx.astype(bf16), dq.astype(bf16), dk.astype(bf16), dv.astype(bf16)

def prologue(states,cot,hist,gain,normed,mcot,inv):
    def body(b,_):
        r=pl.ds(pl.multiple_of(b*S,S),S)
        x=states[r,:].astype(f32)
        iv=lax.rsqrt(jnp.mean(x*x,axis=-1,keepdims=True)+1e-6)
        inv[r,:]=jnp.broadcast_to(iv,(S,128))
        normed[r,:]=((x*iv)*gain[...]).astype(bf16)
        keep=lax.broadcasted_iota(jnp.int32,(S,D),0)<4*hist[b]
        mcot[r,:]=jnp.where(keep,cot[r,:].astype(f32),0.0).astype(bf16)
        return 0
    lax.fori_loop(0,16,body,0)

def block(slot,i,first,hist,wq,wo,normed,mcot,proj,dctx,ctx,gproj,att,gn):
    r0=pl.multiple_of(i*R,R)
    rows=pl.ds(r0,R)
    proj[...]=nt(normed[rows,:],wq[slot]).astype(bf16)
    dctx[...]=nt(mcot[rows,:],wo[slot]).astype(bf16)
    for j in range(NB):
        a=slice(j*S,(j+1)*S)
        c,dq,dk,dv=attend(proj[a,0:256],proj[a,256:512],proj[a,512:768],dctx[a,:],4*hist[i*NB+j])
        rr=pl.ds(pl.multiple_of(r0+j*S,S),S)
        ctx[rr,:]=c
        gproj[rr,0:256]=dq
        gproj[rr,256:512]=dk
        gproj[rr,512:768]=dv
    t=nn(ctx[rows,:],wo[slot])
    att[rows,:]=t if first else att[rows,:]+t
    t=nn(gproj[rows,:],wq[slot])
    gn[rows,:]=t if first else gn[rows,:]+t

def wgrads(normed,mcot,ctx,gproj,g):
    def body(t,_):
        c=pl.ds(pl.multiple_of(t*256,256),256)
        g[c,0:768]=tn(normed[:,c],gproj[...]).astype(g.dtype)
        g[c,768:1024]=tn(mcot[:,c],ctx[...]).astype(g.dtype)
        return 0
    lax.fori_loop(0,3,body,0)

def epilogue(states,gain,mcot,inv,att,gn,attended,gstates,gg):
    gg[...]=jnp.zeros_like(gg)
    def body(b,_):
        r=pl.ds(pl.multiple_of(b*S,S),S)
        x=states[r,:].astype(f32)
        iv=inv[r,0:1]
        attended[r,:]=(x+att[r,:]).astype(bf16)
        u=x*iv
        n=gn[r,:]
        gg[...]+=jnp.sum(n*u,axis=0,keepdims=True)
        gu=n*gain[...]
        m=jnp.mean(gu*u,axis=-1,keepdims=True)
        gstates[r,:]=(mcot[r,:].astype(f32)+iv*(gu-u*m)).astype(bf16)
        return 0
    lax.fori_loop(0,16,body,0)

def kernel(hist,states,cot,gain,wq,wo,attended,gstates,g,gg,normed,mcot,inv,proj,dctx,ctx,gproj,att,gn):
    prologue(states,cot,hist,gain,normed,mcot,inv)
    def b0(i,_):
        block(0,i,True,hist,wq,wo,normed,mcot,proj,dctx,ctx,gproj,att,gn); return 0
    lax.fori_loop(0,16//NB,b0,0)
    wgrads(normed,mcot,ctx,gproj,g)
    def b1(t,_):
        block(1+t//(16//NB),lax.rem(t,16//NB),False,hist,wq,wo,normed,mcot,proj,dctx,ctx,gproj,att,gn); return 0
    lax.fori_loop(0,3*(16//NB),b1,0)
    epilogue(states,gain,mcot,inv,att,gn,attended,gstates,gg)

V=pl.BlockSpec(memory_space=pltpu.VMEM)
def compute(hist,states,cot,gain,wq,wo):
    n=16*S
    return pl.pallas_call(kernel,
        out_shape=(jax.ShapeDtypeStruct((n,D),bf16),jax.ShapeDtypeStruct((n,D),bf16),jax.ShapeDtypeStruct((D,1024),f32),jax.ShapeDtypeStruct((1,D),f32)),
        in_specs=[pl.BlockSpec(memory_space=pltpu.SMEM)]+[V]*5, out_specs=(V,)*4,
        scratch_shapes=[pltpu.VMEM((n,D),bf16),pltpu.VMEM((n,D),bf16),pltpu.VMEM((n,128),f32),
            pltpu.VMEM((R,D),bf16),pltpu.VMEM((R,256),bf16),pltpu.VMEM((n,256),bf16),pltpu.VMEM((n,D),bf16),
            pltpu.VMEM((n,D),f32),pltpu.VMEM((n,D),f32)],
        compiler_params=pltpu.CompilerParams(vmem_limit_bytes=60*2**20),
    )(hist,states,cot,gain,wq,wo)


def summed(x, axis):
    n = lax.axis_size(axis)
    y = lax.all_to_all(x.reshape(n, x.shape[0] // n, x.shape[1]), axis, 0, 0, tiled=True)
    return jnp.sum(y.astype(f32), axis=0)


def body(states, hist_len, norm_gain, qkv_weight, output_weight, cotangent):
    me = lax.axis_index("mp")
    order = lax.rem(me + jnp.arange(4), 4)
    wq = jnp.transpose(qkv_weight, (1, 2, 3, 0))
    wq = lax.all_gather(wq, "mp")[order]
    wo = lax.all_gather(output_weight, "mp")[order]
    wq = jnp.pad(wq, ((0, 0), (0, 0), (0, 1), (0, 0), (0, 0))).reshape(4, 768, 768)
    wo = jnp.pad(wo, ((0, 0), (0, 1), (0, 0), (0, 0))).reshape(4, 256, 768)
    attended, gstates, g, gg = compute(
        hist_len, states.reshape(-1, D), cotangent.reshape(-1, D), norm_gain[None], wq, wo
    )
    g = g.reshape(768, 4, 4, 64)[:, :, :3].reshape(768, 768).astype(bf16)
    g = summed(g, "dp").reshape(12, 4, 3, 64)
    gg = summed(jnp.reshape(gg, (768, 1)).astype(bf16), "dp").reshape(12)
    shape = states.shape
    return (
        attended.reshape(shape),
        gstates.reshape(shape),
        g[:, :3],
        jnp.transpose(g[:, 3], (1, 2, 0)),
        gg,
    )


def solution(mesh):
    placed = (
        P("dp", None, None),
        P("dp"),
        P(),
        P(None, None, "mp", None),
        P("mp", None, None),
        P("dp", None, None),
    )
    return jax.shard_map(
        body,
        mesh=mesh,
        in_specs=placed,
        out_specs=(
            P("dp", None, None),
            P("dp", None, None),
            P("dp", None, "mp", None),
            P("mp", None, "dp"),
            P("dp"),
        ),
        check_vma=False,
    )
```

time: 416 us -> 291 us (0.70)
  waiting for transfers between devices: 232 us -> 154 us
  Pallas kernels: 0 us -> 71.9 us
  local copies, waits for them, and re-layouts: 73.3 us -> 21.7 us
  starting transfers between devices: 61.9 us -> 25.2 us
  matrix products: 25 us -> 0 us
  other arithmetic: 21.6 us -> 3.73 us
  between operations: 1.02 us -> 14.1 us
    all_to_all x9 -> x2, waiting for transfers between devices: 232 us -> 42.8 us  [summed(): lax.all_to_all(x.reshape(n, x.shape[0] // n, x.shape[1]), axis, 0, 0, til...]
    all_gather x0 -> x2, waiting for transfers between devices: none -> 109 us  [the longest x1 70.6 us: body(): wq = lax.all_gather(wq, 'mp')[order]]
    pallas_call x0 -> x1, Pallas kernels: none -> 71.9 us  [compute(): pl.pallas_call(kernel, out_shape=(jax.ShapeDtypeStruct((n, D), bf16), jax...]
    reshape x9 -> x1, local copies, waits for them, and re-layouts: 37.4 us -> 0.1 us  [body(): g = summed(g, 'dp').reshape(12, 4, 3, 64)]
    all_to_all x9 -> x2, starting transfers between devices: 61.9 us -> 25.1 us  [summed(): lax.all_to_all(x.reshape(n, x.shape[0] // n, x.shape[1]), axis, 0, 0, til...]
    dot_general x11 -> x0, matrix products: 21.4 us -> none  [the longest x1 3.41 us: body(): jnp.einsum('bsd,dchk->bschk', normed, qkv_weight, preferred_element_type=...]
    unnamed x41 -> x1, local copies, waits for them, and re-layouts: 18.2 us -> 0.61 us
    reduce_sum x8 -> x2, other arithmetic: 11.7 us -> 0.88 us  [summed(): return jnp.sum(y.astype(f32), axis=0)]
  transfers between devices with their start and end apart: 9 -> 4, of which waited for: 7 -> 3; matrix products, arithmetic and copies ran while one was open for 19% -> 6% of each run, Pallas kernels for 0% -> 0%
where the time goes in v1:
time: 291 us; the launch traced here: 290 us
  waiting for transfers between devices  154 us (53%)
  Pallas kernels  71.9 us (25%)
  starting transfers between devices  25.2 us (9%)
  local copies, waits for them, and re-layouts  21.7 us (7%)
  between operations  14.1 us (5%)
  other arithmetic  3.73 us (1%)
    pallas_call x1, Pallas kernels, compute(): pl.pallas_call(kernel, out_shape=(jax.ShapeDtypeStruct((n, D), bf16), jax...  71.9 us
    all_gather x1, waiting for transfers between devices, body(): wq = lax.all_gather(wq, 'mp')[order]  70.6 us
    all_to_all x2, waiting for transfers between devices, summed(): lax.all_to_all(x.reshape(n, x.shape[0] // n, x.shape[1]), axis, 0, 0, til...  42.8 us
    all_gather x1, waiting for transfers between devices, body(): wo = lax.all_gather(output_weight, 'mp')[order]  38.8 us
    all_to_all x2, starting transfers between devices, summed(): lax.all_to_all(x.reshape(n, x.shape[0] // n, x.shape[1]), axis, 0, 0, til...  25.1 us
  transfers between devices with their start and end apart: 4, of which 3 were waited for; matrix products, arithmetic and copies ran while one was open for 6% of the time, Pallas kernels for 0%

profile of v1, /device:TPU:1, one launch (start us, length us, event | category | flops | bytes accessed | tf_op | source)
XLA Modules:
  0.0 290.2 jit_solution(2548908179256639288)
XLA Ops:
  7.2 0.0 all-gather.7.cloned.1.call-start
  7.2 0.7 all-gather.7.cloned.1.call-update
  7.9 0.0 all-gather.5.cloned.1.call-start
  7.9 0.7 all-gather.5.cloned.1.call-update
  8.7 1.3 broadcast_in_dim.2.gain
  9.9 38.8 %all-gather.7.cloned.1.call-done = bf16[12,64,768]{2,1,0:T(8,128)(2,1)} async-done(((bf16[3,64,768]{2,1,0:T(8,128)(2,1)}), bf16[12,64,768]{2,1,0:T(8,128)(2,1)}) %all-gather.7.cloned.1.call-update) | async-done | bytes 1179664 | tf_op jit(solution)/shard_map/all_gather | solution.py:126
  48.7 1.9 gather_fusion.1
  50.6 1.4 pad.9
  52.0 70.6 %all-gather.5.cloned.1.call-done = bf16[12,3,64,768]{3,2,1,0:T(8,128)(2,1)} async-done(((bf16[3,3,64,768]{3,2,1,0:T(8,128)(2,1)}), bf16[12,3,64,768]{3,2,1,0:T(8,128)(2,1)}) %all-gather.5.cloned.1.call-update) | async-done | bytes 3538960 | tf_op jit(solution)/shard_map/all_gather | solution.py:125
  122.6 2.8 gather_fusion
  125.4 2.6 pad.8
  128.0 71.9 %shard_map.101 = (bf16[1280,768]{1,0:T(8,128)(2,1)}, bf16[1280,768]{1,0:T(8,128)(2,1)}, f32[768,1024]{1,0:T(8,128)}, f32[1,768]{1,0:T(1,128)}) custom-call(s32[16]{0:T(128)} %hist.1, bf16[1280,768]{1,0:T(8,128)(2,1)} %bitcast.20, bf16[1280,768]{1,0:T(8,128)(2,1)} %bitcast.21, f32[1,768]{1,0:T(1,128)} %broadcast_in_dim.2.gain, bf16[4,768,768]{2,1,0:T(8,128)(2,1)} %bitcast.16, ...), custom_call_target="tpu_custom_call" | custom-call | tf_op jit(solution)/shard_map/pallas_call | solution.py:105
  199.9 0.7 convert_reduce_fusion.2
  200.6 0.7 convert_element_type.35
  201.3 12.4 %all-to-all-start.1 = ((bf16[64,12,1]{1,2,0:T(2,128)(2,1)}), bf16[64,12,1]{1,2,0:T(2,128)(2,1)S(1)}, u32[]{:S(2)}, u32[]{:S(2)}) async-start(bf16[64,12,1]{1,2,0:T(2,128)(2,1)} %convert_element_type.35), calls=%async_computation.1 | async-start | bytes 65536 | tf_op jit(solution)/shard_map/all_to_all | solution.py:117
  213.7 2.1 convert.4
  215.9 0.7 copy.15
  216.6 1.1 slice.17
  217.7 4.6 %copy.16 = bf16[768,4,3,64]{3,2,1,0:T(4,128)(2,1)S(1)} copy(bf16[768,4,3,64]{0,3,2,1:T(8,128)(2,1)} %slice.17) | data formatting | bytes 2359296 | tf_op jit(solution)/shard_map/slice | solution.py:132
  222.3 3.3 %convert_element_type.30 = bf16[64,12,768]{2,1,0:T(8,128)(2,1)} reshape(bf16[768,4,3,64]{3,2,1,0:T(4,128)(2,1)S(1)} %copy.16) | data formatting | bytes 2359296 | tf_op jit(solution)/shard_map/convert_element_type | solution.py:132
  225.6 0.0 all-to-all-done.1
  225.6 12.7 %all-to-all-start = ((bf16[64,12,768]{2,1,0:T(8,128)(2,1)}), bf16[64,12,768]{2,1,0:T(8,128)(2,1)S(1)}, u32[]{:S(2)}, u32[]{:S(2)}) async-start(bf16[64,12,768]{2,1,0:T(8,128)(2,1)} %convert_element_type.30), calls=%async_computation | async-start | bytes 3145728 | tf_op jit(solution)/shard_map/all_to_all | solution.py:117
  238.3 0.6 convert_reduce_fusion.1
  238.9 42.8 %all-to-all-done = bf16[64,12,768]{2,1,0:T(8,128)(2,1)S(1)} async-done(((bf16[64,12,768]{2,1,0:T(8,128)(2,1)}), bf16[64,12,768]{2,1,0:T(8,128)(2,1)S(1)}, u32[]{:S(2)}, u32[]{:S(2)}) %all-to-all-start) | async-done | bytes 1179680 | tf_op jit(solution)/shard_map/all_to_all | solution.py:117
  281.7 0.3 convert_reduce_fusion
  282.0 0.1 reshape.99
  282.1 0.6 slice.18
  282.8 0.6 copy.18
  (3 shorter events, 0.0 us)
Async XLA Ops:
  7.2 41.6 %all-gather.7.cloned.1.call-start = ((), (), s32[]{:S(2)}) async-start(), calls=%async_computation.3 | async-start | bytes 1474560 | tf_op jit(solution)/shard_map/all_gather | solution.py:126
  7.9 114.7 %all-gather.5.cloned.1.call-start = ((), (), s32[]{:S(2)}) async-start(), calls=%async_computation.2 | async-start | bytes 4423680 | tf_op jit(solution)/shard_map/all_gather | solution.py:125
  201.3 24.3 %all-to-all-start.1 = ((bf16[64,12,1]{1,2,0:T(2,128)(2,1)}), bf16[64,12,1]{1,2,0:T(2,128)(2,1)S(1)}, u32[]{:S(2)}, u32[]{:S(2)}) async-start(bf16[64,12,1]{1,2,0:T(2,128)(2,1)} %convert_element_type.35), calls=%async_computation.1 | async-start | bytes 65536 | tf_op jit(solution)/shard_map/all_to_all | solution.py:117
  225.6 56.1 %all-to-all-start = ((bf16[64,12,768]{2,1,0:T(8,128)(2,1)}), bf16[64,12,768]{2,1,0:T(8,128)(2,1)S(1)}, u32[]{:S(2)}, u32[]{:S(2)}) async-start(bf16[64,12,768]{2,1,0:T(8,128)(2,1)} %convert_element_type.30), calls=%async_computation | async-start | bytes 3145728 | tf_op jit(solution)/shard_map/all_to_all | solution.py:117
Sparse Core Ops, SparseCore 0:
  9.8 38.8 all-gather.6
  50.5 72.0 all-gather.4

commit v2 on v1

v2 whole, which is shorter than its diff:
```python
import jax, jax.numpy as jnp
from jax import lax
from jax.experimental import pallas as pl
from jax.experimental.pallas import tpu as pltpu
from jax.sharding import PartitionSpec as P

S=80; D=768; NB=4; R=NB*S
f32=jnp.float32; bf16=jnp.bfloat16

def nt(a,b): return lax.dot_general(a,b,(((1,),(1,)),((),())),preferred_element_type=f32)
def nn(a,b): return lax.dot_general(a,b,(((1,),(0,)),((),())),preferred_element_type=f32)
def tn(a,b): return lax.dot_general(a,b,(((0,),(0,)),((),())),preferred_element_type=f32)

def attend(q,k,v,dc,keys):
    lane=lax.broadcasted_iota(jnp.int32,(1,256),1)//64
    ms=[(lane==h).astype(bf16) for h in range(3)]
    mf=[m.astype(f32) for m in ms]
    z=jnp.zeros((16,256),bf16)
    qs=jnp.concatenate([q*m for m in ms]+[z],axis=0)
    dst=jnp.concatenate([dc*m for m in ms]+[z],axis=0)
    st=nt(k,qs)
    keep=lax.broadcasted_iota(jnp.int32,(S,256),0)<keys
    st=jnp.where(keep,st,-1e30)
    e=jnp.exp(st-jnp.max(st,axis=0,keepdims=True))
    p=e*(1.0/jnp.sum(e,axis=0,keepdims=True))
    pb=p.astype(bf16)
    o=tn(pb,v)
    ctx=o[0:S]*mf[0]+o[S:2*S]*mf[1]+o[2*S:3*S]*mf[2]
    dp=nt(v,dst)
    ds=(p*(dp-jnp.sum(p*dp,axis=0,keepdims=True))).astype(bf16)
    dv=nn(pb,dst)
    dk=nn(ds,qs)
    u=tn(ds,k)
    dq=u[0:S]*mf[0]+u[S:2*S]*mf[1]+u[2*S:3*S]*mf[2]
    return ctx.astype(bf16), dq.astype(bf16), dk.astype(bf16), dv.astype(bf16)

def prologue(states,cot,hist,gain,normed,mcot,inv):
    def body(b,_):
        r=pl.ds(pl.multiple_of(b*S,S),S)
        x=states[r,:].astype(f32)
        iv=lax.rsqrt(jnp.mean(x*x,axis=-1,keepdims=True)+1e-6)
        inv[r,:]=jnp.broadcast_to(iv,(S,128))
        normed[r,:]=((x*iv)*gain[...]).astype(bf16)
        keep=lax.broadcasted_iota(jnp.int32,(S,D),0)<4*hist[b]
        mcot[r,:]=jnp.where(keep,cot[r,:].astype(f32),0.0).astype(bf16)
        return 0
    lax.fori_loop(0,16,body,0)

MESH = pl.DeviceIdType.MESH


def block(slot, i, hist, w, normed, mcot, proj, dctx, ctx, gproj, att, gn):
    r0 = pl.multiple_of(i * R, R)
    rows = pl.ds(r0, R)
    proj[...] = nt(normed[rows, :], w[slot, 0:3].reshape(768, D)).astype(bf16)
    dctx[...] = nt(mcot[rows, :], w[slot, 3]).astype(bf16)
    for j in range(NB):
        a = slice(j * S, (j + 1) * S)
        c, dq, dk, dv = attend(
            proj[a, 0:256], proj[a, 256:512], proj[a, 512:768], dctx[a, :], 4 * hist[i * NB + j]
        )
        rr = pl.ds(pl.multiple_of(r0 + j * S, S), S)
        ctx[rr, :] = c
        gproj[rr, 0:256] = dq
        gproj[rr, 256:512] = dk
        gproj[rr, 512:768] = dv
    att[rows, :] += nn(ctx[rows, :], w[slot, 3])
    gn[rows, :] += nn(gproj[rows, :], w[slot, 0:3].reshape(768, D))


def wgrads(normed, mcot, ctx, gproj, gs):
    def body(t, _):
        c = pl.ds(pl.multiple_of(t * 256, 256), 256)
        g = tn(normed[:, c], gproj[...])
        o = tn(mcot[:, c], ctx[...])
        gs[0, c, 0:128] = g[:, 0:128].astype(bf16)
        gs[0, c, 128:256] = g[:, 256:384].astype(bf16)
        gs[0, c, 256:384] = g[:, 512:640].astype(bf16)
        gs[1, c, 0:128] = o[:, 0:128].astype(bf16)
        gs[1, c, 128:256] = (g[:, 128:256] + pltpu.roll(g[:, 384:512], 64, 1)).astype(bf16)
        gs[1, c, 256:384] = (g[:, 640:768] + pltpu.roll(o[:, 128:256], 64, 1)).astype(bf16)
        return 0

    lax.fori_loop(0, 3, body, 0)


def local_gain(states, inv, gn, gg):
    gg[...] = jnp.zeros_like(gg)

    def body(b, _):
        r = pl.ds(pl.multiple_of(b * S, S), S)
        t = gn[r, :] * (states[r, :].astype(f32) * inv[r, 0:1])
        gg[...] += jnp.sum(t.reshape(S // 8, 8, D), axis=0)
        return 0

    lax.fori_loop(0, 16, body, 0)


def epilogue(states, gain, mcot, inv, att, gn, attended, gstates):
    def body(b, _):
        r = pl.ds(pl.multiple_of(b * S, S), S)
        x = states[r, :].astype(f32)
        iv = inv[r, 0:1]
        attended[r, :] = (x + att[r, :]).astype(bf16)
        u = x * iv
        gu = gn[r, :] * gain[...]
        m = jnp.mean(gu * u, axis=-1, keepdims=True)
        gstates[r, :] = (mcot[r, :].astype(f32) + iv * (gu - u * m)).astype(bf16)
        return 0

    lax.fori_loop(0, 16, body, 0)


def kernel(
    hist, states, cot, gain, wq_hbm, wo_hbm,
    attended, gstates, gq_out, go_out, gg_out,
    w, normed, mcot, inv, proj, dctx, ctx, gproj, att, gn,
    gs, ra, sb, rb, sc, rc, sd, rd, fin, gg, gb,
    load_sem, send_sem, recv_sem,
):
    dp, zl = lax.axis_index("dp"), lax.axis_index("mp")
    x, y, zh, core = dp // 16, lax.rem(dp // 4, 4), lax.rem(dp // 2, 2), lax.rem(dp, 2)
    z = zh * 4 + zl

    def dev(x, y, z, core):
        return (((x * 4 + y) * 2 + z // 4) * 2 + core, lax.rem(z, 4))

    def at_z(k):
        return dev(x, y, lax.rem(z + k, 8), core)

    up, down, up2, down2, far = at_z(1), at_z(7), at_z(2), at_z(6), at_z(4)
    twin = dev(x, y, z, 1 - core)
    xs = [dev(lax.rem(x + k, 4), y, z, core) for k in (1, 2, 3)]
    ys = [dev(x, lax.rem(y + k, 4), z, core) for k in (1, 2, 3)]

    loads = [
        pltpu.make_async_copy(wq_hbm, w.at[0, pl.ds(0, 3), pl.ds(0, 192), :], load_sem.at[0]),
        pltpu.make_async_copy(wo_hbm, w.at[0, 3, pl.ds(0, 192), :], load_sem.at[1]),
    ]
    for c in loads:
        c.start()
    barrier = pltpu.get_barrier_semaphore()
    peers = [up, down, up2, down2, far, twin] + xs + ys
    for p in peers:
        pl.semaphore_signal(barrier, inc=1, device_id=p, device_id_type=MESH)

    count = [0]

    def remote(src, dst, device):
        k = count[0]
        count[0] += 1
        return pltpu.make_async_remote_copy(
            src_ref=src, dst_ref=dst, send_sem=send_sem.at[k], recv_sem=recv_sem.at[k],
            device_id=device, device_id_type=MESH,
        )

    def part(slot, first, n):
        return w.at[slot, pl.ds(first, n), pl.ds(0, 192), :]

    c2 = 2 * core
    to_up = remote(part(0, c2, 2), part(1, c2, 2), up)
    to_down = remote(part(0, c2, 2), part(2, c2, 2), down)
    to_up2 = remote(part(0, c2, 1), part(3, c2, 1), up2)
    to_down2 = remote(part(0, c2 + 1, 1), part(3, c2 + 1, 1), down2)
    pass_on = [remote(part(s, c2, 2), part(s, c2, 2), twin) for s in (1, 2, 3)]
    st_a = [remote(gs.at[1 - core], ra, twin), remote(gg.at[0], gb.at[0], twin)]
    st_b, st_c = [], []
    for k in (1, 2, 3):
        chunk = pl.ds(pl.multiple_of(lax.rem(x + k, 4) * 192, 192), 192)
        st_b.append(remote(sb.at[chunk, :], rb.at[k - 1], xs[k - 1]))
        st_b.append(remote(gg.at[1], gb.at[k], xs[k - 1]))
    for k in (1, 2, 3):
        chunk = pl.ds(pl.multiple_of(lax.rem(y + k, 4) * 48, 48), 48)
        st_c.append(remote(sc.at[chunk, :], rc.at[k - 1], ys[k - 1]))
        st_c.append(remote(gg.at[2], gb.at[3 + k], ys[k - 1]))
    st_d = [remote(sd.at[0], rd, far), remote(gg.at[3], gb.at[7], far)]
    st_e = [remote(sd.at[1], fin.at[core], twin)]
    st_e += [remote(gg.at[4], gb.at[8 + k], d) for k, d in enumerate((up, down, up2))]

    def start(cs):
        for c in cs:
            c.start()

    def wait(cs):
        for c in cs:
            c.wait()

    for s in range(4):
        for p in range(4):
            w[s, p, 192:256, :] = jnp.zeros((64, D), bf16)
    att[...] = jnp.zeros_like(att)
    gn[...] = jnp.zeros_like(gn)
    for c in loads:
        c.wait()
    pl.semaphore_wait(barrier, len(peers))
    start([to_up, to_down, to_up2, to_down2])
    prologue(states, cot, hist, gain, normed, mcot, inv)

    def step(t, _):
        slot = t // (16 // NB)
        i = lax.rem(t, 16 // NB)

        @pl.when(t == 4)
        def _():
            pass_on[0].wait()

        @pl.when(t == 8)
        def _():
            pass_on[1].wait()

        @pl.when(t == 12)
        def _():
            pass_on[2].wait()

        block(slot, i, hist, w, normed, mcot, proj, dctx, ctx, gproj, att, gn)

        @pl.when(t == 3)
        def _():
            to_up.wait()
            pass_on[0].start()
            to_down.wait()
            pass_on[1].start()
            wgrads(normed, mcot, ctx, gproj, gs)
            local_gain(states, inv, gn, gg.at[0])
            start(st_a)

        @pl.when(t == 4)
        def _():
            wait(st_a)
            sb[...] = (gs[core].astype(f32) + ra[...].astype(f32)).astype(bf16)
            gg[1] = gg[0] + gb[0]

        @pl.when(t == 5)
        def _():
            start(st_b)

        @pl.when(t == 7)
        def _():
            to_up2.wait()
            to_down2.wait()
            pass_on[2].start()
            wait(st_b)
            own = sb[pl.ds(pl.multiple_of(x * 192, 192), 192), :].astype(f32)
            for k in range(3):
                own += rb[k].astype(f32)
            sc[...] = own.astype(bf16)
            gg[2] = gg[1] + (gb[1] + gb[2] + gb[3])

        @pl.when(t == 8)
        def _():
            start(st_c)

        @pl.when(t == 9)
        def _():
            wait(st_c)
            own = sc[pl.ds(pl.multiple_of(y * 48, 48), 48), :].astype(f32)
            for k in range(3):
                own += rc[k].astype(f32)
            sd[0] = own.astype(bf16)
            gg[3] = gg[2] + (gb[4] + gb[5] + gb[6])

        @pl.when(t == 10)
        def _():
            start(st_d)

        @pl.when(t == 11)
        def _():
            wait(st_d)
            both = (sd[0].astype(f32) + rd[...].astype(f32)).astype(bf16)
            sd[1] = both
            fin[core] = both
            gg[4] = gg[3] + gb[7]

        @pl.when(t == 12)
        def _():
            start(st_e)

        @pl.when(t == 13)
        def _():
            wait(st_e)
            total = gg[4] + (gb[8] + gb[9] + gb[10])
            total = jnp.sum(total, axis=0, keepdims=True)
            total = jnp.broadcast_to(total, (8, D))
            gg_out[...] = pltpu.roll(total, lax.rem(D - 12 * dp, D), 1)[0:1, 0:12]
            mine = 12 * (2 * zh + core)
            pad = jnp.zeros((80, 384), f32)
            for h in range(2):
                rows = jnp.concatenate([fin[h].astype(f32), pad], axis=0).T
                cols = pltpu.roll(rows, lax.rem(128 - mine, 128), 1)[:, 0:12]
                if h == 0:
                    for c in range(3):
                        gq_out[192 * c : 192 * c + 128, :] = cols[128 * c : 128 * c + 128]
                else:
                    go_out[0:128, :] = cols[0:128]
                    for c in range(3):
                        gq_out[192 * c + 128 : 192 * c + 192, :] = cols[128 + 64 * c : 192 + 64 * c]
                    go_out[128:192, :] = cols[320:384]

        return 0

    lax.fori_loop(0, 64 // NB, step, 0)
    epilogue(states, gain, mcot, inv, att, gn, attended, gstates)


VMEM = pl.BlockSpec(memory_space=pltpu.VMEM)
ANY = pl.BlockSpec(memory_space=pl.ANY)
COPIES = 29


def compute(hist, states, cot, gain, wq, wo):
    n = 16 * S
    return pl.pallas_call(
        kernel,
        out_shape=(
            jax.ShapeDtypeStruct((n, D), bf16),
            jax.ShapeDtypeStruct((n, D), bf16),
            jax.ShapeDtypeStruct((576, 12), f32),
            jax.ShapeDtypeStruct((192, 12), f32),
            jax.ShapeDtypeStruct((1, 12), f32),
        ),
        in_specs=[pl.BlockSpec(memory_space=pltpu.SMEM), VMEM, VMEM, VMEM, ANY, ANY],
        out_specs=(VMEM,) * 5,
        scratch_shapes=[
            pltpu.VMEM((4, 4, 256, D), bf16),
            pltpu.VMEM((n, D), bf16),
            pltpu.VMEM((n, D), bf16),
            pltpu.VMEM((n, 128), f32),
            pltpu.VMEM((R, D), bf16),
            pltpu.VMEM((R, 256), bf16),
            pltpu.VMEM((n, 256), bf16),
            pltpu.VMEM((n, D), bf16),
            pltpu.VMEM((n, D), f32),
            pltpu.VMEM((n, D), f32),
            pltpu.VMEM((2, D, 384), bf16),
            pltpu.VMEM((D, 384), bf16),
            pltpu.VMEM((D, 384), bf16),
            pltpu.VMEM((3, 192, 384), bf16),
            pltpu.VMEM((192, 384), bf16),
            pltpu.VMEM((3, 48, 384), bf16),
            pltpu.VMEM((2, 48, 384), bf16),
            pltpu.VMEM((48, 384), bf16),
            pltpu.VMEM((2, 48, 384), bf16),
            pltpu.VMEM((5, 8, D), f32),
            pltpu.VMEM((11, 8, D), f32),
            pltpu.SemaphoreType.DMA((2,)),
            pltpu.SemaphoreType.DMA((COPIES,)),
            pltpu.SemaphoreType.DMA((COPIES,)),
        ],
        compiler_params=pltpu.CompilerParams(
            vmem_limit_bytes=60 * 2**20, collective_id=0, has_side_effects=True
        ),
    )(hist, states, cot, gain, wq, wo)


def body(states, hist_len, norm_gain, qkv_weight, output_weight, cotangent):
    wq = jnp.transpose(qkv_weight, (1, 2, 3, 0)).reshape(3, 192, D)
    wo = output_weight.reshape(192, D)
    attended, gstates, gq, go, gg = compute(
        hist_len, states.reshape(-1, D), cotangent.reshape(-1, D), norm_gain[None], wq, wo
    )
    shape = states.shape
    return (
        attended.reshape(shape),
        gstates.reshape(shape),
        jnp.transpose(gq.reshape(3, 3, 64, 12), (3, 0, 1, 2)),
        go.reshape(3, 64, 12),
        gg.reshape(12),
    )


def solution(mesh):
    placed = (
        P("dp", None, None),
        P("dp"),
        P(),
        P(None, None, "mp", None),
        P("mp", None, None),
        P("dp", None, None),
    )
    return jax.shard_map(
        body,
        mesh=mesh,
        in_specs=placed,
        out_specs=(
            P("dp", None, None),
            P("dp", None, None),
            P("dp", None, "mp", None),
            P("mp", None, "dp"),
            P("dp"),
        ),
        check_vma=False,
    )
```

time: 291 us -> 98.8 us (0.34)
  the two profiles are of different devices: /device:TPU:1 before, /device:TPU:32 now
where the time goes in v2:
time: 98.8 us; the launch traced here: 98.6 us
  Pallas kernels  88.5 us (90%)
  local copies, waits for them, and re-layouts  9.5 us (10%)
    pallas_call x1, Pallas kernels, compute(): pl.pallas_call(kernel, out_shape=(jax.ShapeDtypeStruct((n, D), bf16), jax...  88.5 us
    unnamed x8, local copies, waits for them, and re-layouts  6.47 us

profile of v2, /device:TPU:32, one launch (start us, length us, event | category | flops | bytes accessed | tf_op | source)
XLA Modules:
  0.0 98.6 jit_solution(2957791985912364328)
XLA Ops:
  0.6 1.3 %broadcast_in_dim.3.gain = f32[1,768]{1,0:T(1,128)} reshape(f32[768]{0:T(1024)} %param.8) | data formatting | bytes 6144 | tf_op jit(solution)/shard_map/broadcast_in_dim | solution.py:359
  1.9 88.5 %shard_map.101 = (bf16[1280,768]{1,0:T(8,128)(2,1)}, bf16[1280,768]{1,0:T(8,128)(2,1)}, f32[576,12]{1,0:T(8,128)}, f32[192,12]{1,0:T(8,128)}, f32[1,12]{1,0:T(1,128)}) custom-call(s32[16]{0:T(128)} %hist.1, bf16[1280,768]{1,0:T(8,128)(2,1)} %bitcast.12, bf16[1280,768]{1,0:T(8,128)(2,1)} %bitcast.13, f32[1,768]{1,0:T(1,128)} %broadcast_in_dim.3.gain, ...), custom_call_target="tpu_custom_call" | custom-call | tf_op jit(solution)/shard_map/pallas_call | solution.py:312
  90.4 1.6 %copy.12 = f32[3,64,12]{1,2,0:T(8,128)} copy(f32[3,64,12]{2,1,0:T(8,128)} %bitcast.19) | data formatting | bytes 18432
  92.0 1.8 %copy.11 = f32[3,3,64,12]{2,1,0,3:T(4,128)} copy(f32[3,3,64,12]{3,2,1,0:T(8,128)} %bitcast.17) | data formatting | bytes 55296 | tf_op jit(solution)/shard_map/reshape | solution.py:365
  93.7 0.0 copy-start
  93.7 3.1 %copy.16 = bf16[16,80,768]{2,1,0:T(8,128)(2,1)} copy(bf16[16,80,768]{2,1,0:T(8,128)(2,1)} %bitcast.15) | data formatting | bytes 3932160
  96.8 0.0 copy-done
  96.8 0.0 copy-start.1
  96.8 1.3 %copy.17 = bf16[16,80,768]{2,1,0:T(8,128)(2,1)} copy(bf16[16,80,768]{2,1,0:T(8,128)(2,1)S(1)} %bitcast.14) | data formatting | bytes 3932160
  98.1 0.0 copy-done.1
  98.1 0.5 copy.18
Async XLA Ops:
  93.7 3.1 %copy-start = (bf16[1280,768]{1,0:T(8,128)(2,1)S(1)}, bf16[1280,768]{1,0:T(8,128)(2,1)}, u32[]{:S(2)}) copy-start(bf16[1280,768]{1,0:T(8,128)(2,1)} %get-tuple-element.11) | copy-start | bytes 5898244
  96.8 1.3 %copy-start.1 = (f32[1,12]{1,0:T(1,128)S(1)}, f32[1,12]{1,0:T(1,128)}, u32[]{:S(2)}) copy-start(f32[1,12]{1,0:T(1,128)} %get-tuple-element.14) | copy-start | bytes 148

commit v3 on v2

v3 whole, which is shorter than its diff:
```python
import jax, jax.numpy as jnp
from jax import lax
from jax.experimental import pallas as pl
from jax.experimental.pallas import tpu as pltpu
from jax.sharding import PartitionSpec as P

S=80; D=768; NB=4; R=NB*S; PER=16//NB
f32=jnp.float32; bf16=jnp.bfloat16

def nt(a,b): return lax.dot_general(a,b,(((1,),(1,)),((),())),preferred_element_type=f32)
def nn(a,b): return lax.dot_general(a,b,(((1,),(0,)),((),())),preferred_element_type=f32)
def tn(a,b): return lax.dot_general(a,b,(((0,),(0,)),((),())),preferred_element_type=f32)

def prologue(states,cot,hist,gain,normed,mcot,inv):
    def body(b,_):
        r=pl.ds(pl.multiple_of(b*S,S),S)
        x=states[r,:].astype(f32)
        iv=lax.rsqrt(jnp.mean(x*x,axis=-1,keepdims=True)+1e-6)
        inv[r,:]=jnp.broadcast_to(iv,(S,128))
        normed[r,:]=((x*iv)*gain).astype(bf16)
        keep=lax.broadcasted_iota(jnp.int32,(S,D),0)<4*hist[b]
        mcot[r,:]=jnp.where(keep,cot[r,:].astype(f32),0.0).astype(bf16)
        return 0
    lax.fori_loop(0,16,body,0)

MESH = pl.DeviceIdType.MESH


def fill(t, w, normed, mcot, kb, vb, qs, dcs):
    slot = jnp.minimum(t // (PER), 3)
    buf = lax.rem(t, 2)
    rows = pl.ds(pl.multiple_of(lax.rem(t, PER) * R, R), R)
    low = lax.broadcasted_iota(jnp.int32, (S, 128), 1) < 64
    pr = nt(normed[rows, :], w[slot, 0:3].reshape(768, D))
    dc = nt(mcot[rows, :], w[slot, 3])

    def stack(ref, j, v):
        lo = v[:, 0:128]
        ref[buf, j, 0:S, 0:128] = jnp.where(low, lo, 0.0).astype(bf16)
        ref[buf, j, S : 2 * S, 0:128] = jnp.where(low, 0.0, lo).astype(bf16)
        ref[buf, j, 2 * S : 3 * S, 128:256] = v[:, 128:256].astype(bf16)

    for j in range(NB):
        a = slice(j * S, (j + 1) * S)
        stack(qs, j, pr[a, 0:256])
        kb[buf, j] = pr[a, 256:512].astype(bf16)
        vb[buf, j] = pr[a, 512:768].astype(bf16)
        stack(dcs, j, dc[a])


def push(t, w, ctx, gproj, att, gn):
    slot = t // (PER)
    rows = pl.ds(pl.multiple_of(lax.rem(t, PER) * R, R), R)
    att[rows, :] += nn(ctx[rows, :], w[slot, 3])
    gn[rows, :] += nn(gproj[rows, :], w[slot, 0:3].reshape(768, D))


def attend(t, hist, w, kb, vb, qs, dcs, ctx, gproj, att, gn):
    buf = lax.rem(t, 2)
    i = lax.rem(t, PER)
    row = lax.broadcasted_iota(jnp.int32, (S, 256), 0)
    low = lax.broadcasted_iota(jnp.int32, (S, 128), 1) < 64
    st = [nt(kb[buf, j], qs[buf, j]) for j in range(NB)]
    dp = [nt(vb[buf, j], dcs[buf, j]) for j in range(NB)]
    push(t - 1 + jnp.where(t == 0, PER, 0), w, ctx, gproj, att, gn)
    pb, ds = [], []
    for j in range(NB):
        x = jnp.where(row < 4 * hist[i * NB + j], st[j], -1e30)
        e = jnp.exp(x - jnp.max(x, axis=0, keepdims=True))
        p = e * (1.0 / jnp.sum(e, axis=0, keepdims=True))
        pb.append(p.astype(bf16))
        pd = p * dp[j]
        ds.append((pd - p * jnp.sum(pd, axis=0, keepdims=True)).astype(bf16))

    def heads(o):
        return jnp.where(low, o[0:S, 0:128], o[S : 2 * S, 0:128]).astype(bf16), o[
            2 * S : 3 * S, 128:256
        ].astype(bf16)

    for j in range(NB):
        rr = pl.ds(pl.multiple_of((i * NB + j) * S, S), S)
        ctx[rr, 0:128], ctx[rr, 128:256] = heads(tn(pb[j], vb[buf, j]))
        gproj[rr, 0:128], gproj[rr, 128:256] = heads(tn(ds[j], kb[buf, j]))
        gproj[rr, 256:512] = nn(ds[j], qs[buf, j]).astype(bf16)
        gproj[rr, 512:768] = nn(pb[j], dcs[buf, j]).astype(bf16)


def wgrads(normed, mcot, ctx, gproj, gs):
    def body(t, _):
        c = pl.ds(pl.multiple_of(t * 256, 256), 256)
        g = tn(normed[:, c], gproj[...])
        o = tn(mcot[:, c], ctx[...])
        gs[0, c, 0:128] = g[:, 0:128].astype(bf16)
        gs[0, c, 128:256] = g[:, 256:384].astype(bf16)
        gs[0, c, 256:384] = g[:, 512:640].astype(bf16)
        gs[1, c, 0:128] = o[:, 0:128].astype(bf16)
        gs[1, c, 128:256] = (g[:, 128:256] + pltpu.roll(g[:, 384:512], 64, 1)).astype(bf16)
        gs[1, c, 256:384] = (g[:, 640:768] + pltpu.roll(o[:, 128:256], 64, 1)).astype(bf16)
        return 0

    lax.fori_loop(0, 3, body, 0)


def local_gain(states, inv, gn, gg):
    gg[...] = jnp.zeros_like(gg)

    def body(b, _):
        r = pl.ds(pl.multiple_of(b * S, S), S)
        t = gn[r, :] * (states[r, :].astype(f32) * inv[r, 0:1])
        gg[...] += jnp.sum(t.reshape(S // 8, 8, D), axis=0)
        return 0

    lax.fori_loop(0, 16, body, 0)


def epilogue(states, gain, mcot, inv, att, gn, attended, gstates):
    def body(b, _):
        r = pl.ds(pl.multiple_of(b * S, S), S)
        x = states[r, :].astype(f32)
        iv = inv[r, 0:1]
        attended[r, :] = (x + att[r, :]).astype(bf16)
        u = x * iv
        gu = gn[r, :] * gain
        m = jnp.mean(gu * u, axis=-1, keepdims=True)
        gstates[r, :] = (mcot[r, :].astype(f32) + iv * (gu - u * m)).astype(bf16)
        return 0

    lax.fori_loop(0, 16, body, 0)


def kernel(
    hist, states_hbm, cot_hbm, gain_hbm, wq_hbm, wo_hbm,
    attended, gstates, gq_out, go_out, gg_out,
    states, cot, gain, w, normed, mcot, inv, kb, vb, qs, dcs, ctx, gproj, att, gn,
    gs, ra, sb, rb, sc, rc, sd, rd, fin, rows, gg, gb,
    load_sem, send_sem, recv_sem,
):
    dp, zl = lax.axis_index("dp"), lax.axis_index("mp")
    x, y, zh, core = dp // 16, lax.rem(dp // 4, 4), lax.rem(dp // 2, 2), lax.rem(dp, 2)
    z = zh * 4 + zl

    def dev(x, y, z, core):
        return (((x * 4 + y) * 2 + z // 4) * 2 + core, lax.rem(z, 4))

    def at_z(k):
        return dev(x, y, lax.rem(z + k, 8), core)

    up, down, up2, down2, far = at_z(1), at_z(7), at_z(2), at_z(6), at_z(4)
    twin = dev(x, y, z, 1 - core)
    xs = [dev(lax.rem(x + k, 4), y, z, core) for k in (1, 2, 3)]
    ys = [dev(x, lax.rem(y + k, 4), z, core) for k in (1, 2, 3)]

    loads = [
        pltpu.make_async_copy(wq_hbm, w.at[0, pl.ds(0, 3), pl.ds(0, 192), :], load_sem.at[0]),
        pltpu.make_async_copy(wo_hbm, w.at[0, 3, pl.ds(0, 192), :], load_sem.at[1]),
        pltpu.make_async_copy(gain_hbm, gain, load_sem.at[2]),
        pltpu.make_async_copy(states_hbm, states, load_sem.at[3]),
        pltpu.make_async_copy(cot_hbm, cot, load_sem.at[4]),
    ]
    for c in loads:
        c.start()
    barrier = pltpu.get_barrier_semaphore()
    peers = [up, down, up2, down2, far, twin] + xs + ys
    for p in peers:
        pl.semaphore_signal(barrier, inc=1, device_id=p, device_id_type=MESH)

    count = [0]

    def remote(src, dst, device):
        k = count[0]
        count[0] += 1
        return pltpu.make_async_remote_copy(
            src_ref=src, dst_ref=dst, send_sem=send_sem.at[k], recv_sem=recv_sem.at[k],
            device_id=device, device_id_type=MESH,
        )

    def part(slot, first, n):
        return w.at[slot, pl.ds(first, n), pl.ds(0, 192), :]

    c2 = 2 * core
    to_up = remote(part(0, c2, 2), part(1, c2, 2), up)
    to_down = remote(part(0, c2, 2), part(2, c2, 2), down)
    to_up2 = remote(part(0, c2, 1), part(3, c2, 1), up2)
    to_down2 = remote(part(0, c2 + 1, 1), part(3, c2 + 1, 1), down2)
    pass_on = [remote(part(s, c2, 2), part(s, c2, 2), twin) for s in (1, 2, 3)]
    st_a = [remote(gs.at[1 - core], ra, twin), remote(gg.at[0], gb.at[0], twin)]
    st_b, st_c = [], []
    for k in (1, 2, 3):
        chunk = pl.ds(pl.multiple_of(lax.rem(x + k, 4) * 192, 192), 192)
        st_b.append(remote(sb.at[chunk, :], rb.at[k - 1], xs[k - 1]))
        st_b.append(remote(gg.at[1], gb.at[k], xs[k - 1]))
    for k in (1, 2, 3):
        chunk = pl.ds(pl.multiple_of(lax.rem(y + k, 4) * 48, 48), 48)
        st_c.append(remote(sc.at[chunk, :], rc.at[k - 1], ys[k - 1]))
        st_c.append(remote(gg.at[2], gb.at[3 + k], ys[k - 1]))
    st_d = [remote(sd.at[0], rd, far), remote(gg.at[3], gb.at[7], far)]
    st_e = [remote(sd.at[1], fin.at[core], twin)]
    st_e += [remote(gg.at[4], gb.at[8 + k], d) for k, d in enumerate((up, down, up2))]

    def start(cs):
        for c in cs:
            c.start()

    def wait(cs):
        for c in cs:
            c.wait()

    for s in range(4):
        for p in range(4):
            w[s, p, 192:256, :] = jnp.zeros((64, D), bf16)
    for r in (qs, dcs, ctx, gproj, att, gn):
        r[...] = jnp.zeros_like(r)
    for c in loads[0:2]:
        c.wait()
    pl.semaphore_wait(barrier, len(peers))
    start([to_up, to_down, to_up2, to_down2])
    for c in loads[2:]:
        c.wait()
    gain = gain[...].reshape(1, D)
    prologue(states, cot, hist, gain, normed, mcot, inv)

    fill(0, w, normed, mcot, kb, vb, qs, dcs)

    def early(t, _):
        attend(t, hist, w, kb, vb, qs, dcs, ctx, gproj, att, gn)
        fill(t + 1, w, normed, mcot, kb, vb, qs, dcs)
        return 0

    lax.fori_loop(0, PER - 1, early, 0)
    attend(PER - 1, hist, w, kb, vb, qs, dcs, ctx, gproj, att, gn)
    wgrads(normed, mcot, ctx, gproj, gs)
    to_up.wait()
    pass_on[0].start()
    to_down.wait()
    pass_on[1].start()
    st_a[0].start()
    pass_on[0].wait()
    fill(PER, w, normed, mcot, kb, vb, qs, dcs)

    def step(t, _):
        @pl.when(t == 7)
        def _():
            pass_on[1].wait()

        @pl.when(t == 11)
        def _():
            pass_on[2].wait()

        attend(t, hist, w, kb, vb, qs, dcs, ctx, gproj, att, gn)
        fill(t + 1, w, normed, mcot, kb, vb, qs, dcs)

        @pl.when(t == 4)
        def _():
            local_gain(states, inv, gn, gg.at[0])

        @pl.when(t == 5)
        def _():
            st_a[1].start()
            st_a[0].wait()
            sb[...] = (gs[core].astype(f32) + ra[...].astype(f32)).astype(bf16)

        @pl.when(t == 6)
        def _():
            start(st_b[0::2])
            st_a[1].wait()
            gg[1] = gg[0] + gb[0]

        @pl.when(t == 7)
        def _():
            start(st_b[1::2])

        @pl.when(t == 8)
        def _():
            wait(st_b)
            own = sb[pl.ds(pl.multiple_of(x * 192, 192), 192), :].astype(f32)
            for k in range(3):
                own += rb[k].astype(f32)
            sc[...] = own.astype(bf16)
            gg[2] = gg[1] + (gb[1] + gb[2] + gb[3])

        @pl.when(t == 9)
        def _():
            start(st_c)
            to_up2.wait()
            to_down2.wait()
            pass_on[2].start()

        @pl.when(t == 10)
        def _():
            wait(st_c)
            own = sc[pl.ds(pl.multiple_of(y * 48, 48), 48), :].astype(f32)
            for k in range(3):
                own += rc[k].astype(f32)
            sd[0] = own.astype(bf16)
            gg[3] = gg[2] + (gb[4] + gb[5] + gb[6])

        @pl.when(t == 11)
        def _():
            start(st_d)

        @pl.when(t == 12)
        def _():
            wait(st_d)
            both = (sd[0].astype(f32) + rd[...].astype(f32)).astype(bf16)
            sd[1] = both
            fin[core] = both
            gg[4] = gg[3] + gb[7]

        @pl.when(t == 13)
        def _():
            start(st_e)

        @pl.when(t == 14)
        def _():
            wait(st_e)
            total = gg[4] + (gb[8] + gb[9] + gb[10])
            total = jnp.sum(total, axis=0, keepdims=True)
            total = jnp.broadcast_to(total, (8, D))
            gg_out[...] = pltpu.roll(total, lax.rem(D - 12 * dp, D), 1)[0:1, 0:12]
            for h in range(2):
                part_h = fin[h].astype(f32)
                for q in range(4):
                    rows[q, 0:12, 384 * h : 384 * h + 384] = part_h[12 * q : 12 * q + 12]
            mine = rows[2 * zh + core, 0:12, :]
            for r in range(12):
                one = mine[r : r + 1]
                for c in range(3):
                    at = 512 + 64 * c
                    gq_out[r, c, 0:1, :] = one[:, 128 * c : 128 * c + 64]
                    gq_out[r, c, 1:2, :] = one[:, 128 * c + 64 : 128 * c + 128]
                    gq_out[r, c, 2:3, :] = one[:, at : at + 64]
            go_out[0] = mine[:, 384:448]
            go_out[1] = mine[:, 448:512]
            go_out[2] = mine[:, 704:768]

        return 0

    lax.fori_loop(PER, 4 * PER - 1, step, 0)
    attend(4 * PER - 1, hist, w, kb, vb, qs, dcs, ctx, gproj, att, gn)
    push(4 * PER - 1, w, ctx, gproj, att, gn)
    epilogue(states, gain, mcot, inv, att, gn, attended, gstates)


VMEM = pl.BlockSpec(memory_space=pltpu.VMEM)
HBM = pl.BlockSpec(memory_space=pltpu.MemorySpace.HBM)
COPIES = 27


def compute(hist, states, cot, gain, wq, wo):
    n = 16 * S
    return pl.pallas_call(
        kernel,
        out_shape=(
            jax.ShapeDtypeStruct((n, D), bf16),
            jax.ShapeDtypeStruct((n, D), bf16),
            jax.ShapeDtypeStruct((12, 3, 3, 64), f32),
            jax.ShapeDtypeStruct((3, 12, 64), f32),
            jax.ShapeDtypeStruct((1, 12), f32),
        ),
        in_specs=[pl.BlockSpec(memory_space=pltpu.SMEM)] + [HBM] * 5,
        out_specs=(VMEM,) * 5,
        scratch_shapes=[
            pltpu.VMEM((n, D), bf16),
            pltpu.VMEM((n, D), bf16),
            pltpu.VMEM((D,), f32),
            pltpu.VMEM((4, 4, 256, D), bf16),
            pltpu.VMEM((n, D), bf16),
            pltpu.VMEM((n, D), bf16),
            pltpu.VMEM((n, 128), f32),
            pltpu.VMEM((2, NB, S, 256), bf16),
            pltpu.VMEM((2, NB, S, 256), bf16),
            pltpu.VMEM((2, NB, 256, 256), bf16),
            pltpu.VMEM((2, NB, 256, 256), bf16),
            pltpu.VMEM((n, 256), bf16),
            pltpu.VMEM((n, D), bf16),
            pltpu.VMEM((n, D), f32),
            pltpu.VMEM((n, D), f32),
            pltpu.VMEM((2, D, 384), bf16),
            pltpu.VMEM((D, 384), bf16),
            pltpu.VMEM((D, 384), bf16),
            pltpu.VMEM((3, 192, 384), bf16),
            pltpu.VMEM((192, 384), bf16),
            pltpu.VMEM((3, 48, 384), bf16),
            pltpu.VMEM((2, 48, 384), bf16),
            pltpu.VMEM((48, 384), bf16),
            pltpu.VMEM((2, 48, 384), bf16),
            pltpu.VMEM((4, 16, D), f32),
            pltpu.VMEM((5, 8, D), f32),
            pltpu.VMEM((11, 8, D), f32),
            pltpu.SemaphoreType.DMA((5,)),
            pltpu.SemaphoreType.DMA((COPIES,)),
            pltpu.SemaphoreType.DMA((COPIES,)),
        ],
        compiler_params=pltpu.CompilerParams(
            vmem_limit_bytes=40 * 2**20, collective_id=0, has_side_effects=True
        ),
    )(*[pltpu.with_memory_space_constraint(v, pltpu.HBM) for v in (hist, states, cot, gain, wq, wo)])


def put_kernel(*refs):
    n = len(refs) // 2
    sem = refs[-1]
    copies = [pltpu.make_async_copy(refs[k], refs[n + k], sem.at[k]) for k in range(n)]
    for c in copies:
        c.start()
    for c in copies:
        c.wait()


def put(arrays):
    return pl.pallas_call(
        put_kernel,
        out_shape=tuple(jax.ShapeDtypeStruct(a.shape, a.dtype) for a in arrays),
        in_specs=[VMEM] * len(arrays),
        out_specs=(HBM,) * len(arrays),
        scratch_shapes=[pltpu.SemaphoreType.DMA((len(arrays),))],
        compiler_params=pltpu.CompilerParams(vmem_limit_bytes=2**20),
    )(*arrays)


def body(states, hist_len, norm_gain, qkv_weight, output_weight, cotangent):
    wq = jnp.transpose(qkv_weight, (1, 2, 3, 0)).reshape(3, 192, D)
    wo = output_weight.reshape(192, D)
    attended, gstates, gq, go, gg = put(
        compute(hist_len, states.reshape(-1, D), cotangent.reshape(-1, D), norm_gain, wq, wo)
    )
    shape = states.shape
    return (
        attended.reshape(shape),
        gstates.reshape(shape),
        gq,
        jnp.transpose(go, (0, 2, 1)),
        gg.reshape(12),
    )


def solution(mesh):
    placed = (
        P("dp", None, None),
        P("dp"),
        P(),
        P(None, None, "mp", None),
        P("mp", None, None),
        P("dp", None, None),
    )
    return jax.shard_map(
        body,
        mesh=mesh,
        in_specs=placed,
        out_specs=(
            P("dp", None, None),
            P("dp", None, None),
            P("dp", None, "mp", None),
            P("mp", None, "dp"),
            P("dp"),
        ),
        check_vma=False,
    )
```

time: 98.8 us -> 75.9 us (0.77)
  the two profiles are of different devices: /device:TPU:32 before, /device:TPU:1 now
where the time goes in v3:
time: 75.9 us; the launch traced here: 75.3 us
  Pallas kernels  74.6 us (98%)
    pallas_call x1, Pallas kernels, compute(): pl.pallas_call(kernel, out_shape=(jax.ShapeDtypeStruct((n, D), bf16), jax...  72.6 us
    pallas_call x1, Pallas kernels, put(): pl.pallas_call(put_kernel, out_shape=tuple((jax.ShapeDtypeStruct(a.shape,...  1.97 us

profile of v3, /device:TPU:1, one launch (start us, length us, event | category | flops | bytes accessed | tf_op | source)
XLA Modules:
  0.0 75.3 jit_solution(8159255630987022901)
XLA Ops:
  0.6 72.6 %shard_map.101 = (bf16[1280,768]{1,0:T(8,128)(2,1)S(1)}, bf16[1280,768]{1,0:T(8,128)(2,1)S(1)}, f32[12,3,3,64]{3,2,1,0:T(4,128)S(1)}, f32[3,12,64]{2,1,0:T(8,128)S(1)}, f32[1,12]{1,0:T(1,128)S(1)}) custom-call(s32[16]{0:T(128)} %hist.1, bf16[1280,768]{1,0:T(8,128)(2,1)} %bitcast.10, bf16[1280,768]{1,0:T(8,128)(2,1)} %bitcast.11, f32[768]{0:T(1024)} %gain_hbm.1, ...), custom_call_target="tpu_custom_call" | custom-call | tf_op jit(solution)/shard_map/pallas_call | solution.py:351
  73.3 2.0 %shard_map.102 = (bf16[1280,768]{1,0:T(8,128)(2,1)}, bf16[1280,768]{1,0:T(8,128)(2,1)}, f32[12,3,3,64]{3,2,1,0:T(4,128)}, f32[3,12,64]{2,1,0:T(8,128)}, f32[1,12]{1,0:T(1,128)}) custom-call(bf16[1280,768]{1,0:T(8,128)(2,1)S(1)} %get-tuple-element.15.refs_0_, bf16[1280,768]{1,0:T(8,128)(2,1)S(1)} %get-tuple-element.16.refs_1_, ...), custom_call_target="tpu_custom_call" | custom-call | tf_op jit(solution)/shard_map/pallas_call | solution.py:411

commit v4 on v3

v4 whole, which is shorter than its diff:
```python
import jax
import jax.numpy as jnp
from jax import lax
from jax.experimental import pallas as pl
from jax.experimental.pallas import tpu as pltpu
from jax.sharding import PartitionSpec as P

S = 80
D = 768
NB = 4
R = NB * S
PER = 16 // NB
f32 = jnp.float32
bf16 = jnp.bfloat16
PARTS = ((3,), (0,), (1,), (2,), (4, 5))
MESH = pl.DeviceIdType.MESH


def dot(a, b, ca, cb):
    return lax.dot_general(a, b, (((ca,), (cb,)), ((), ())), preferred_element_type=f32)


def nt(a, b):
    return dot(a, b, 1, 1)


def nn(a, b):
    return dot(a, b, 1, 0)


def tn(a, b):
    return dot(a, b, 0, 0)


def block_rows(t):
    return pl.ds(pl.multiple_of(lax.rem(t, PER) * R, R), R)


def prologue(i, states, cot, hist, gain, normed, mcot, inv):
    for j in range(NB):
        b = i * NB + j
        r = pl.ds(pl.multiple_of(b * S, S), S)
        x = states[r, :].astype(f32)
        iv = lax.rsqrt(jnp.mean(x * x, axis=-1, keepdims=True) + 1e-6)
        inv[r, :] = jnp.broadcast_to(iv, (S, 128))
        normed[r, :] = ((x * iv) * gain[...].reshape(1, D)).astype(bf16)
        keep = lax.broadcasted_iota(jnp.int32, (S, D), 0) < 4 * hist[b]
        mcot[r, :] = jnp.where(keep, cot[r, :].astype(f32), 0.0).astype(bf16)


def fill(t, w, normed, mcot, kb, vb, qs, dcs):
    slot = t // PER
    buf = lax.rem(t, 2)
    rows = block_rows(t)
    low = lax.broadcasted_iota(jnp.int32, (S, 128), 1) < 64

    def stack(ref, j, v):
        lo = v[:, 0:128]
        ref[buf, j, 0:S, 0:128] = jnp.where(low, lo, 0.0).astype(bf16)
        ref[buf, j, S : 2 * S, 0:128] = jnp.where(low, 0.0, lo).astype(bf16)
        ref[buf, j, 2 * S : 3 * S, 128:256] = v[:, 128:256].astype(bf16)

    for c in range(4):
        v = nt((mcot if c == 3 else normed)[rows, :], w[slot, c])
        for j in range(NB):
            one = v[j * S : (j + 1) * S]
            if c == 0:
                stack(qs, j, one)
            elif c == 3:
                stack(dcs, j, one)
            else:
                (kb if c == 1 else vb)[buf, j] = one.astype(bf16)


def push_part(t, n, w, ctx, gproj, att, gn):
    slot = t // PER
    rows = block_rows(t)
    c = slice(256 * (n % 3), 256 * (n % 3) + 256)
    if n < 3:
        att[rows, c] += nn(ctx[rows, :], w[slot, 3, :, c])
    else:
        gn[rows, c] += nn(gproj[rows, :], w[slot, 0:3, :, c].reshape(768, 256))


def push(t, *refs):
    for n in range(6):
        push_part(t, n, *refs)


def attend(t, hist, w, kb, vb, qs, dcs, ctx, gproj, att, gn):
    buf = lax.rem(t, 2)
    i = lax.rem(t, PER)
    row = lax.broadcasted_iota(jnp.int32, (S, 256), 0)
    low = lax.broadcasted_iota(jnp.int32, (S, 128), 1) < 64
    before = t - 1 + jnp.where(t == 0, PER, 0)
    pb, ds = [], []
    for n in PARTS[0]:
        push_part(before, n, w, ctx, gproj, att, gn)
    for j in range(NB):
        st = nt(kb[buf, j], qs[buf, j])
        dp = nt(vb[buf, j], dcs[buf, j])
        for n in PARTS[j + 1]:
            push_part(before, n, w, ctx, gproj, att, gn)
        x = jnp.where(row < 4 * hist[i * NB + j], st, -1e30)
        e = jnp.exp(x - jnp.max(x, axis=0, keepdims=True))
        p = e * (1.0 / jnp.sum(e, axis=0, keepdims=True))
        pb.append(p.astype(bf16))
        pd = p * dp
        ds.append((pd - p * jnp.sum(pd, axis=0, keepdims=True)).astype(bf16))

    def heads(o):
        two = jnp.where(low, o[0:S, 0:128], o[S : 2 * S, 0:128])
        return two.astype(bf16), o[2 * S : 3 * S, 128:256].astype(bf16)

    for j in range(NB):
        rr = pl.ds(pl.multiple_of((i * NB + j) * S, S), S)
        ctx[rr, 0:128], ctx[rr, 128:256] = heads(tn(pb[j], vb[buf, j]))
        gproj[rr, 512:768] = nn(pb[j], dcs[buf, j]).astype(bf16)
        gproj[rr, 0:128], gproj[rr, 128:256] = heads(tn(ds[j], kb[buf, j]))
        gproj[rr, 256:512] = nn(ds[j], qs[buf, j]).astype(bf16)


def wgrads(normed, mcot, ctx, gproj, gs):
    def body(t, _):
        c = pl.ds(pl.multiple_of(t * 256, 256), 256)
        g = tn(normed[:, c], gproj[...])
        o = tn(mcot[:, c], ctx[...])
        gs[0, c, 0:128] = g[:, 0:128].astype(bf16)
        gs[0, c, 128:256] = g[:, 256:384].astype(bf16)
        gs[0, c, 256:384] = g[:, 512:640].astype(bf16)
        gs[1, c, 0:128] = o[:, 0:128].astype(bf16)
        gs[1, c, 128:256] = (g[:, 128:256] + pltpu.roll(g[:, 384:512], 64, 1)).astype(bf16)
        gs[1, c, 256:384] = (g[:, 640:768] + pltpu.roll(o[:, 128:256], 64, 1)).astype(bf16)
        return 0

    lax.fori_loop(0, 3, body, 0)


def local_gain(states, inv, gn, gg):
    gg[...] = jnp.zeros_like(gg)

    def body(b, _):
        r = pl.ds(pl.multiple_of(b * S, S), S)
        t = gn[r, :] * (states[r, :].astype(f32) * inv[r, 0:1])
        gg[...] += jnp.sum(t.reshape(S // 8, 8, D), axis=0)
        return 0

    lax.fori_loop(0, 16, body, 0)


def epilogue(i, states, gain, mcot, inv, att, gn, attended, gstates):
    for j in range(NB):
        r = pl.ds(pl.multiple_of((i * NB + j) * S, S), S)
        x = states[r, :].astype(f32)
        iv = inv[r, 0:1]
        attended[r, :] = (x + att[r, :]).astype(bf16)
        u = x * iv
        gu = gn[r, :] * gain[...].reshape(1, D)
        m = iv * jnp.mean(gu * u, axis=-1, keepdims=True)
        gstates[r, :] = (mcot[r, :].astype(f32) + (iv * gu - u * m)).astype(bf16)


def kernel(
    hist, states_hbm, cot_hbm, gain_hbm, wq_hbm, wo_hbm,
    attended, gstates, gq_out, go_out, gg_out,
    states, cot, gain, w, normed, mcot, inv, kb, vb, qs, dcs, ctx, gproj, att, gn,
    gs, ra, sb, rb, sc, rc, sd, rd, fin, rows, gg, gb,
    load_sem, send_sem, recv_sem,
):
    dp, zl = lax.axis_index("dp"), lax.axis_index("mp")
    x, y, zh, core = dp // 16, lax.rem(dp // 4, 4), lax.rem(dp // 2, 2), lax.rem(dp, 2)
    z = zh * 4 + zl

    def dev(x, y, z, core):
        return (((x * 4 + y) * 2 + z // 4) * 2 + core, lax.rem(z, 4))

    def at_z(k):
        return dev(x, y, lax.rem(z + k, 8), core)

    up, down, up2, down2, far = at_z(1), at_z(7), at_z(2), at_z(6), at_z(4)
    twin = dev(x, y, z, 1 - core)
    xs = [dev(lax.rem(x + k, 4), y, z, core) for k in (1, 2, 3)]
    ys = [dev(x, lax.rem(y + k, 4), z, core) for k in (1, 2, 3)]

    def load(k, src, dst):
        return pltpu.make_async_copy(src, dst, load_sem.at[k])

    w_loads = [
        load(0, wq_hbm, w.at[0, pl.ds(0, 3), pl.ds(0, 192), :]),
        load(1, wo_hbm, w.at[0, 3, pl.ds(0, 192), :]),
    ]
    gain_load = load(2, gain_hbm, gain)
    x_loads = []
    for i in range(PER):
        r = pl.ds(i * R, R)
        x_loads.append(load(3 + 2 * i, states_hbm.at[r, :], states.at[r, :]))
        x_loads.append(load(4 + 2 * i, cot_hbm.at[r, :], cot.at[r, :]))

    def start(cs):
        for c in cs:
            c.start()

    def wait(cs):
        for c in cs:
            c.wait()

    start(w_loads)
    barrier = pltpu.get_barrier_semaphore()
    peers = [up, down, up2, down2, far, twin] + xs + ys
    for p in peers:
        pl.semaphore_signal(barrier, inc=1, device_id=p, device_id_type=MESH)
    gain_load.start()
    start(x_loads)

    count = [0]

    def remote(src, dst, device):
        k = count[0]
        count[0] += 1
        return pltpu.make_async_remote_copy(
            src_ref=src, dst_ref=dst, send_sem=send_sem.at[k], recv_sem=recv_sem.at[k],
            device_id=device, device_id_type=MESH,
        )

    def part(slot, first, n, at=0, size=192):
        return w.at[slot, pl.ds(first, n), pl.ds(at, size), :]

    def head(slot, k):
        return part(slot, c2, 2, 64 * k, 64)

    c2 = 2 * core
    near = [
        remote(head(0, 0), head(1, 0), up), remote(head(0, 0), head(1, 2), down),
        remote(head(0, 1), head(1, 1), up), remote(head(0, 1), head(2, 0), down),
        remote(head(0, 2), head(2, 2), up), remote(head(0, 2), head(2, 1), down),
    ]
    opposite = [
        remote(part(0, c2, 1), part(3, c2, 1), up2),
        remote(part(0, c2 + 1, 1), part(3, c2 + 1, 1), down2),
    ]
    pass_1 = [remote(head(1, k), head(1, k), twin) for k in (0, 2, 1)]
    pass_2 = remote(part(2, c2, 2), part(2, c2, 2), twin)
    pass_3 = remote(part(3, c2, 2), part(3, c2, 2), twin)

    g_a, n_a = remote(gs.at[1 - core], ra, twin), remote(gg.at[0], gb.at[0], twin)
    g_b, n_b, g_c, n_c = [], [], [], []
    for k in (1, 2, 3):
        chunk = pl.ds(pl.multiple_of(lax.rem(x + k, 4) * 192, 192), 192)
        g_b.append(remote(sb.at[chunk, :], rb.at[k - 1], xs[k - 1]))
        n_b.append(remote(gg.at[1], gb.at[k], xs[k - 1]))
        chunk = pl.ds(pl.multiple_of(lax.rem(y + k, 4) * 48, 48), 48)
        g_c.append(remote(sc.at[chunk, :], rc.at[k - 1], ys[k - 1]))
        n_c.append(remote(gg.at[2], gb.at[3 + k], ys[k - 1]))
    d_all = [remote(sd.at[0], rd, far), remote(gg.at[3], gb.at[7], far)]
    e_all = [remote(sd.at[1], fin.at[core], twin)]
    e_all += [remote(gg.at[4], gb.at[8 + k], d) for k, d in enumerate((up, down, up2))]

    for p in range(4):
        w[0, p, 192:256, :] = jnp.zeros((64, D), bf16)
    wait(w_loads)
    pl.semaphore_wait(barrier, len(peers))
    start(near)
    start(opposite)
    for s in range(1, 4):
        for p in range(4):
            w[s, p, 192:256, :] = jnp.zeros((64, D), bf16)
    for r in (qs, dcs, ctx, gproj, att, gn):
        r[...] = jnp.zeros_like(r)
    gain_load.wait()
    wait(x_loads)

    pro = (states, cot, hist, gain, normed, mcot, inv)
    fil = (w, normed, mcot, kb, vb, qs, dcs)
    atn = (hist, w, kb, vb, qs, dcs, ctx, gproj, att, gn)
    epi = (states, gain, mcot, inv, att, gn, attended, gstates)

    prologue(0, *pro)
    fill(0, *fil)
    prologue(1, *pro)

    def early(t, _):
        attend(t, *atn)
        fill(t + 1, *fil)
        prologue(jnp.minimum(t + 2, PER - 1), *pro)
        return 0

    lax.fori_loop(0, PER - 1, early, 0)
    wait(near[0:2])
    start(pass_1[0:2])
    attend(PER - 1, *atn)
    wgrads(normed, mcot, ctx, gproj, gs)
    near[2].wait()
    pass_1[2].start()
    g_a.start()
    wait(pass_1)
    fill(PER, *fil)

    def step(t, _):
        @pl.when(t == 7)
        def _():
            pass_2.wait()

        @pl.when(t == 11)
        def _():
            pass_3.wait()

        attend(t, *atn)
        fill(t + 1, *fil)

        @pl.when(t == 4)
        def _():
            local_gain(states, inv, gn, gg.at[0])
            wait(near[3:6])
            pass_2.start()

        @pl.when(t == 5)
        def _():
            n_a.start()
            g_a.wait()
            sb[...] = (gs[core].astype(f32) + ra[...].astype(f32)).astype(bf16)

        @pl.when(t == 6)
        def _():
            start(g_b)
            n_a.wait()
            gg[1] = gg[0] + gb[0]

        @pl.when(t == 7)
        def _():
            start(n_b)

        @pl.when(t == 9)
        def _():
            wait(g_b)
            wait(n_b)
            own = sb[pl.ds(pl.multiple_of(x * 192, 192), 192), :].astype(f32)
            for k in range(3):
                own += rb[k].astype(f32)
            sc[...] = own.astype(bf16)
            gg[2] = gg[1] + (gb[1] + gb[2] + gb[3])
            wait(opposite)
            pass_3.start()

        @pl.when(t == 10)
        def _():
            start(g_c)
            start(n_c)

        @pl.when(t == 11)
        def _():
            wait(g_c)
            wait(n_c)
            own = sc[pl.ds(pl.multiple_of(y * 48, 48), 48), :].astype(f32)
            for k in range(3):
                own += rc[k].astype(f32)
            sd[0] = own.astype(bf16)
            gg[3] = gg[2] + (gb[4] + gb[5] + gb[6])

        @pl.when(t == 12)
        def _():
            start(d_all)

        return 0

    lax.fori_loop(PER, 3 * PER + 1, step, 0)

    def late(t, _):
        attend(t, *atn)
        fill(t + 1, *fil)
        epilogue(lax.rem(t - 1, PER), *epi)

        @pl.when(t == 3 * PER + 1)
        def _():
            wait(d_all)
            both = (sd[0].astype(f32) + rd[...].astype(f32)).astype(bf16)
            sd[1] = both
            fin[core] = both
            gg[4] = gg[3] + gb[7]

        return 0

    lax.fori_loop(3 * PER + 1, 4 * PER - 1, late, 0)
    start(e_all)
    attend(4 * PER - 1, *atn)
    epilogue(PER - 2, *epi)
    wait(e_all)
    push(4 * PER - 1, w, ctx, gproj, att, gn)
    total = gg[4] + (gb[8] + gb[9] + gb[10])
    total = jnp.broadcast_to(jnp.sum(total, axis=0, keepdims=True), (8, D))
    gg_out[...] = pltpu.roll(total, lax.rem(D - 12 * dp, D), 1)[0:1, 0:12]
    for h in range(2):
        part_h = fin[h].astype(f32)
        for q in range(4):
            rows[q, 0:12, 384 * h : 384 * h + 384] = part_h[12 * q : 12 * q + 12]
    mine = rows[2 * zh + core, 0:12, :]
    for r in range(12):
        one = mine[r : r + 1]
        for c in range(3):
            at = 512 + 64 * c
            gq_out[r, c, 0:1, :] = one[:, 128 * c : 128 * c + 64]
            gq_out[r, c, 1:2, :] = one[:, 128 * c + 64 : 128 * c + 128]
            gq_out[r, c, 2:3, :] = one[:, at : at + 64]
    go_out[0] = mine[:, 384:448]
    go_out[1] = mine[:, 448:512]
    go_out[2] = mine[:, 704:768]
    epilogue(PER - 1, *epi)


VMEM = pl.BlockSpec(memory_space=pltpu.VMEM)
HBM = pl.BlockSpec(memory_space=pltpu.MemorySpace.HBM)
COPIES = 33


def in_hbm(*arrays):
    return [pltpu.with_memory_space_constraint(a, pltpu.HBM) for a in arrays]


def compute(*args):
    n = 16 * S

    def rows_of(width, kind, *lead):
        return pltpu.VMEM((*lead, n, width), kind)

    return pl.pallas_call(
        kernel,
        out_shape=(
            jax.ShapeDtypeStruct((n, D), bf16),
            jax.ShapeDtypeStruct((n, D), bf16),
            jax.ShapeDtypeStruct((12, 3, 3, 64), f32),
            jax.ShapeDtypeStruct((3, 12, 64), f32),
            jax.ShapeDtypeStruct((1, 12), f32),
        ),
        in_specs=[pl.BlockSpec(memory_space=pltpu.SMEM)] + [HBM] * 5,
        out_specs=(VMEM,) * 5,
        scratch_shapes=[
            rows_of(D, bf16),
            rows_of(D, bf16),
            pltpu.VMEM((D,), f32),
            pltpu.VMEM((4, 4, 256, D), bf16),
            rows_of(D, bf16),
            rows_of(D, bf16),
            rows_of(128, f32),
            pltpu.VMEM((2, NB, S, 256), bf16),
            pltpu.VMEM((2, NB, S, 256), bf16),
            pltpu.VMEM((2, NB, 256, 256), bf16),
            pltpu.VMEM((2, NB, 256, 256), bf16),
            rows_of(256, bf16),
            rows_of(D, bf16),
            rows_of(D, f32),
            rows_of(D, f32),
            pltpu.VMEM((2, D, 384), bf16),
            pltpu.VMEM((D, 384), bf16),
            pltpu.VMEM((D, 384), bf16),
            pltpu.VMEM((3, 192, 384), bf16),
            pltpu.VMEM((192, 384), bf16),
            pltpu.VMEM((3, 48, 384), bf16),
            pltpu.VMEM((2, 48, 384), bf16),
            pltpu.VMEM((48, 384), bf16),
            pltpu.VMEM((2, 48, 384), bf16),
            pltpu.VMEM((4, 16, D), f32),
            pltpu.VMEM((5, 8, D), f32),
            pltpu.VMEM((11, 8, D), f32),
            pltpu.SemaphoreType.DMA((3 + 2 * PER,)),
            pltpu.SemaphoreType.DMA((COPIES,)),
            pltpu.SemaphoreType.DMA((COPIES,)),
        ],
        compiler_params=pltpu.CompilerParams(
            vmem_limit_bytes=44 * 2**20, collective_id=0, has_side_effects=True
        ),
    )(*in_hbm(*args))


def put_kernel(*refs):
    n = len(refs) // 2
    sem = refs[-1]
    copies = [pltpu.make_async_copy(refs[k], refs[n + k], sem.at[k]) for k in range(n)]
    for c in copies:
        c.start()
    for c in copies:
        c.wait()


def put(arrays):
    return pl.pallas_call(
        put_kernel,
        out_shape=tuple(jax.ShapeDtypeStruct(a.shape, a.dtype) for a in arrays),
        in_specs=[VMEM] * len(arrays),
        out_specs=(HBM,) * len(arrays),
        scratch_shapes=[pltpu.SemaphoreType.DMA((len(arrays),))],
        compiler_params=pltpu.CompilerParams(vmem_limit_bytes=2**20),
    )(*arrays)


def body(states, hist_len, norm_gain, qkv_weight, output_weight, cotangent):
    wq = jnp.transpose(qkv_weight, (1, 2, 3, 0)).reshape(3, 192, D)
    wo = output_weight.reshape(192, D)
    attended, gstates, gq, go, gg = put(
        compute(hist_len, states.reshape(-1, D), cotangent.reshape(-1, D), norm_gain, wq, wo)
    )
    shape = states.shape
    return (
        attended.reshape(shape),
        gstates.reshape(shape),
        gq,
        jnp.transpose(go, (0, 2, 1)),
        gg.reshape(12),
    )


def solution(mesh):
    placed = (
        P("dp", None, None),
        P("dp"),
        P(),
        P(None, None, "mp", None),
        P("mp", None, None),
        P("dp", None, None),
    )
    return jax.shard_map(
        body,
        mesh=mesh,
        in_specs=placed,
        out_specs=(
            P("dp", None, None),
            P("dp", None, None),
            P("dp", None, "mp", None),
            P("mp", None, "dp"),
            P("dp"),
        ),
        check_vma=False,
    )
```

time: 75.9 us -> 66.3 us (0.87)
  Pallas kernels: 74.6 us -> 64.6 us
    pallas_call x1, Pallas kernels: 72.6 us -> 62.7 us  [compute(): pl.pallas_call(kernel, out_shape=(jax.ShapeDtypeStruct((n, D), bf16), jax...]
where the time goes in v4:
time: 66.3 us; the launch traced here: 65.3 us
  Pallas kernels  64.6 us (97%)
    pallas_call x1, Pallas kernels, compute(): pl.pallas_call(kernel, out_shape=(jax.ShapeDtypeStruct((n, D), bf16), jax...  62.7 us
    pallas_call x1, Pallas kernels, put(): pl.pallas_call(put_kernel, out_shape=tuple((jax.ShapeDtypeStruct(a.shape,...  1.97 us

profile of v4, /device:TPU:1, one launch (start us, length us, event | category | flops | bytes accessed | tf_op | source)
XLA Modules:
  0.0 65.3 jit_solution(13943792771566489992)
XLA Ops:
  0.6 62.7 %shard_map.101 = (bf16[1280,768]{1,0:T(8,128)(2,1)S(1)}, bf16[1280,768]{1,0:T(8,128)(2,1)S(1)}, f32[12,3,3,64]{3,2,1,0:T(4,128)S(1)}, f32[3,12,64]{2,1,0:T(8,128)S(1)}, f32[1,12]{1,0:T(1,128)S(1)}) custom-call(s32[16]{0:T(128)} %hist.1, bf16[1280,768]{1,0:T(8,128)(2,1)} %bitcast.10, bf16[1280,768]{1,0:T(8,128)(2,1)} %bitcast.11, f32[768]{0:T(1024)} %gain_hbm.1, ...), custom_call_target="tpu_custom_call" | custom-call | tf_op jit(solution)/shard_map/pallas_call | solution.py:424
  63.3 2.0 %shard_map.102 = (bf16[1280,768]{1,0:T(8,128)(2,1)}, bf16[1280,768]{1,0:T(8,128)(2,1)}, f32[12,3,3,64]{3,2,1,0:T(4,128)}, f32[3,12,64]{2,1,0:T(8,128)}, f32[1,12]{1,0:T(1,128)}) custom-call(bf16[1280,768]{1,0:T(8,128)(2,1)S(1)} %get-tuple-element.15.refs_0_, bf16[1280,768]{1,0:T(8,128)(2,1)S(1)} %get-tuple-element.16.refs_1_, ...), custom_call_target="tpu_custom_call" | custom-call | tf_op jit(solution)/shard_map/pallas_call | solution.py:484

commit v5 on v4

--- a/solution.py
+++ b/solution.py
@@ -179,8 +179,12 @@
 
     up, down, up2, down2, far = at_z(1), at_z(7), at_z(2), at_z(6), at_z(4)
     twin = dev(x, y, z, 1 - core)
-    xs = [dev(lax.rem(x + k, 4), y, z, core) for k in (1, 2, 3)]
-    ys = [dev(x, lax.rem(y + k, 4), z, core) for k in (1, 2, 3)]
+    far_twin = dev(x, y, lax.rem(z + 4, 8), 1 - core)
+    c1 = 1 - core
+    first = [dev(lax.rem(x + k * c1, 4), lax.rem(y + k * core, 4), z, core) for k in (1, 2, 3)]
+    second = [dev(lax.rem(x + k * core, 4), lax.rem(y + k * c1, 4), z, core) for k in (1, 2, 3)]
+    one, two = x * c1 + y * core, x * core + y * c1
+    column = [at_z(k) for k in range(1, 8)]
 
     def load(k, src, dst):
         return pltpu.make_async_copy(src, dst, load_sem.at[k])
@@ -206,7 +210,7 @@
 
     start(w_loads)
     barrier = pltpu.get_barrier_semaphore()
-    peers = [up, down, up2, down2, far, twin] + xs + ys
+    peers = [twin, far_twin] + column + first + second
     for p in peers:
         pl.semaphore_signal(barrier, inc=1, device_id=p, device_id_type=MESH)
     gain_load.start()
@@ -245,15 +249,12 @@
     g_a, n_a = remote(gs.at[1 - core], ra, twin), remote(gg.at[0], gb.at[0], twin)
     g_b, n_b, g_c, n_c = [], [], [], []
     for k in (1, 2, 3):
-        chunk = pl.ds(pl.multiple_of(lax.rem(x + k, 4) * 192, 192), 192)
-        g_b.append(remote(sb.at[chunk, :], rb.at[k - 1], xs[k - 1]))
-        n_b.append(remote(gg.at[1], gb.at[k], xs[k - 1]))
-        chunk = pl.ds(pl.multiple_of(lax.rem(y + k, 4) * 48, 48), 48)
-        g_c.append(remote(sc.at[chunk, :], rc.at[k - 1], ys[k - 1]))
-        n_c.append(remote(gg.at[2], gb.at[3 + k], ys[k - 1]))
-    d_all = [remote(sd.at[0], rd, far), remote(gg.at[3], gb.at[7], far)]
-    e_all = [remote(sd.at[1], fin.at[core], twin)]
-    e_all += [remote(gg.at[4], gb.at[8 + k], d) for k, d in enumerate((up, down, up2))]
+        g_b.append(remote(sb.at[lax.rem(one + k, 4)], rb.at[k - 1], first[k - 1]))
+        n_b.append(remote(gg.at[1], gb.at[k], first[k - 1]))
+        g_c.append(remote(sc.at[lax.rem(two + k, 4)], rc.at[k - 1], second[k - 1]))
+        n_c.append(remote(gg.at[2], gb.at[3 + k], second[k - 1]))
+    g_d = [remote(sd, rd.at[k], p) for k, p in enumerate((far, twin, far_twin))]
+    n_d = [remote(gg.at[3], gb.at[6 + k], p) for k, p in enumerate(column, 1)]
 
     for p in range(4):
         w[0, p, 192:256, :] = jnp.zeros((64, D), bf16)
@@ -309,56 +310,55 @@
 
         @pl.when(t == 4)
         def _():
+            g_a.wait()
+            for i in range(4):
+                for j in range(4):
+                    r = slice(192 * i + 48 * j, 192 * i + 48 * j + 48)
+                    both = gs[core, r, :].astype(f32) + ra[r, :].astype(f32)
+                    sb[i * c1 + j * core, i * core + j * c1] = both.astype(bf16)
             local_gain(states, inv, gn, gg.at[0])
+            start(g_b)
+            n_a.start()
             wait(near[3:6])
             pass_2.start()
 
         @pl.when(t == 5)
         def _():
-            n_a.start()
-            g_a.wait()
-            sb[...] = (gs[core].astype(f32) + ra[...].astype(f32)).astype(bf16)
-
-        @pl.when(t == 6)
-        def _():
-            start(g_b)
             n_a.wait()
             gg[1] = gg[0] + gb[0]
 
-        @pl.when(t == 7)
+        @pl.when(t == 6)
         def _():
             start(n_b)
 
-        @pl.when(t == 9)
+        @pl.when(t == 8)
         def _():
             wait(g_b)
-            wait(n_b)
-            own = sb[pl.ds(pl.multiple_of(x * 192, 192), 192), :].astype(f32)
+            own = sb[one].astype(f32)
             for k in range(3):
                 own += rb[k].astype(f32)
             sc[...] = own.astype(bf16)
+            wait(n_b)
             gg[2] = gg[1] + (gb[1] + gb[2] + gb[3])
+            start(g_c)
+            start(n_c)
+
+        @pl.when(t == 9)
+        def _():
             wait(opposite)
             pass_3.start()
 
         @pl.when(t == 10)
         def _():
-            start(g_c)
-            start(n_c)
-
-        @pl.when(t == 11)
-        def _():
             wait(g_c)
-            wait(n_c)
-            own = sc[pl.ds(pl.multiple_of(y * 48, 48), 48), :].astype(f32)
+            own = sc[two].astype(f32)
             for k in range(3):
                 own += rc[k].astype(f32)
-            sd[0] = own.astype(bf16)
+            sd[...] = own.astype(bf16)
+            wait(n_c)
             gg[3] = gg[2] + (gb[4] + gb[5] + gb[6])
-
-        @pl.when(t == 12)
-        def _():
-            start(d_all)
+            start(g_d)
+            start(n_d)
 
         return 0
 
@@ -368,38 +368,32 @@
         attend(t, *atn)
         fill(t + 1, *fil)
         epilogue(lax.rem(t - 1, PER), *epi)
-
-        @pl.when(t == 3 * PER + 1)
-        def _():
-            wait(d_all)
-            both = (sd[0].astype(f32) + rd[...].astype(f32)).astype(bf16)
-            sd[1] = both
-            fin[core] = both
-            gg[4] = gg[3] + gb[7]
-
         return 0
 
     lax.fori_loop(3 * PER + 1, 4 * PER - 1, late, 0)
-    start(e_all)
     attend(4 * PER - 1, *atn)
     epilogue(PER - 2, *epi)
-    wait(e_all)
     push(4 * PER - 1, w, ctx, gproj, att, gn)
-    total = gg[4] + (gb[8] + gb[9] + gb[10])
+    wait(g_d)
+    wait(n_d)
+    total = gg[3]
+    for k in range(1, 8):
+        total += gb[6 + k]
     total = jnp.broadcast_to(jnp.sum(total, axis=0, keepdims=True), (8, D))
     gg_out[...] = pltpu.roll(total, lax.rem(D - 12 * dp, D), 1)[0:1, 0:12]
+    fin[core] = sd[...].astype(f32) + rd[0].astype(f32)
+    fin[c1] = rd[1].astype(f32) + rd[2].astype(f32)
     for h in range(2):
-        part_h = fin[h].astype(f32)
         for q in range(4):
-            rows[q, 0:12, 384 * h : 384 * h + 384] = part_h[12 * q : 12 * q + 12]
+            rows[q, 0:12, 384 * h : 384 * h + 384] = fin[h, 12 * q : 12 * q + 12, :]
     mine = rows[2 * zh + core, 0:12, :]
     for r in range(12):
-        one = mine[r : r + 1]
+        line = mine[r : r + 1]
         for c in range(3):
             at = 512 + 64 * c
-            gq_out[r, c, 0:1, :] = one[:, 128 * c : 128 * c + 64]
-            gq_out[r, c, 1:2, :] = one[:, 128 * c + 64 : 128 * c + 128]
-            gq_out[r, c, 2:3, :] = one[:, at : at + 64]
+            gq_out[r, c, 0:1, :] = line[:, 128 * c : 128 * c + 64]
+            gq_out[r, c, 1:2, :] = line[:, 128 * c + 64 : 128 * c + 128]
+            gq_out[r, c, 2:3, :] = line[:, at : at + 64]
     go_out[0] = mine[:, 384:448]
     go_out[1] = mine[:, 448:512]
     go_out[2] = mine[:, 704:768]
@@ -408,7 +402,7 @@
 
 VMEM = pl.BlockSpec(memory_space=pltpu.VMEM)
 HBM = pl.BlockSpec(memory_space=pltpu.MemorySpace.HBM)
-COPIES = 33
+COPIES = 37
 
 
 def in_hbm(*arrays):
@@ -450,16 +444,16 @@
             rows_of(D, f32),
             pltpu.VMEM((2, D, 384), bf16),
             pltpu.VMEM((D, 384), bf16),
-            pltpu.VMEM((D, 384), bf16),
-            pltpu.VMEM((3, 192, 384), bf16),
-            pltpu.VMEM((192, 384), bf16),
+            pltpu.VMEM((4, 4, 48, 384), bf16),
+            pltpu.VMEM((3, 4, 48, 384), bf16),
+            pltpu.VMEM((4, 48, 384), bf16),
             pltpu.VMEM((3, 48, 384), bf16),
-            pltpu.VMEM((2, 48, 384), bf16),
             pltpu.VMEM((48, 384), bf16),
-            pltpu.VMEM((2, 48, 384), bf16),
+            pltpu.VMEM((3, 48, 384), bf16),
+            pltpu.VMEM((2, 48, 384), f32),
             pltpu.VMEM((4, 16, D), f32),
-            pltpu.VMEM((5, 8, D), f32),
-            pltpu.VMEM((11, 8, D), f32),
+            pltpu.VMEM((4, 8, D), f32),
+            pltpu.VMEM((14, 8, D), f32),
             pltpu.SemaphoreType.DMA((3 + 2 * PER,)),
             pltpu.SemaphoreType.DMA((COPIES,)),
             pltpu.SemaphoreType.DMA((COPIES,)),

time: 66.3 us -> 54.8 us (0.83); the launches traced: 65.3 us -> 54.7 us
  Pallas kernels: 64.6 us -> 54.1 us
    pallas_call x1, Pallas kernels: 62.7 us -> 52.1 us  [compute(): pl.pallas_call(kernel, out_shape=(jax.ShapeDtypeStruct((n, D), bf16), jax...]
where the time goes in v5:
time: 54.8 us; the launch traced here: 54.7 us
  Pallas kernels  54.1 us (99%)
  between operations  0.64 us (1%)
    pallas_call x1, Pallas kernels, compute(): pl.pallas_call(kernel, out_shape=(jax.ShapeDtypeStruct((n, D), bf16), jax...  52.1 us
    pallas_call x1, Pallas kernels, put(): pl.pallas_call(put_kernel, out_shape=tuple((jax.ShapeDtypeStruct(a.shape,...  1.97 us

profile of v5, /device:TPU:1, one launch (start us, length us, event | category | flops | bytes accessed | tf_op | source)
XLA Modules:
  0.0 54.7 jit_solution(8335121177168178225)
XLA Ops:
  0.6 52.1 %shard_map.101 = (bf16[1280,768]{1,0:T(8,128)(2,1)S(1)}, bf16[1280,768]{1,0:T(8,128)(2,1)S(1)}, f32[12,3,3,64]{3,2,1,0:T(4,128)S(1)}, f32[3,12,64]{2,1,0:T(8,128)S(1)}, f32[1,12]{1,0:T(1,128)S(1)}) custom-call(s32[16]{0:T(128)} %hist.1, bf16[1280,768]{1,0:T(8,128)(2,1)} %bitcast.10, bf16[1280,768]{1,0:T(8,128)(2,1)} %bitcast.11, f32[768]{0:T(1024)} %gain_hbm.1, ...), custom_call_target="tpu_custom_call" | custom-call | tf_op jit(solution)/shard_map/pallas_call | solution.py:418
  52.7 2.0 %shard_map.102 = (bf16[1280,768]{1,0:T(8,128)(2,1)}, bf16[1280,768]{1,0:T(8,128)(2,1)}, f32[12,3,3,64]{3,2,1,0:T(4,128)}, f32[3,12,64]{2,1,0:T(8,128)}, f32[1,12]{1,0:T(1,128)}) custom-call(bf16[1280,768]{1,0:T(8,128)(2,1)S(1)} %get-tuple-element.15.refs_0_, bf16[1280,768]{1,0:T(8,128)(2,1)S(1)} %get-tuple-element.16.refs_1_, ...), custom_call_target="tpu_custom_call" | custom-call | tf_op jit(solution)/shard_map/pallas_call | solution.py:478
